TPU v7x, 1024 devices: a whole 4x8x16 slice. The times are simulated.
1024 devices in a mesh: fsdp: 64 (over z, x), row: 16 (over y, core).
Axes of the slice: x: 4, y: 8, z: 16, core: 2. Of those that a mesh axis runs over, the one named last changes fastest.
Arguments:
- weight: bfloat16 [8192, 26624], P('row', 'fsdp'), may hold values from -0.3125 to 0.3125
- momentum: bfloat16 [8192, 26624], P('row', 'fsdp'), may hold values from -6 to 6
- gradient: bfloat16 [8192, 26624], P('row', 'fsdp'), may hold values from -6 to 6
- basis: bfloat16 [26624, 256], P('fsdp'), may hold values from -0.0390625 to 0.0390625
Outputs:
- weight_new: bfloat16 [8192, 26624], P('row', 'fsdp')
- momentum_new: bfloat16 [8192, 26624], P('row', 'fsdp')
- basis_new: bfloat16 [26624, 256], P('fsdp')
All inputs are finite; a program needn't handle non-finite values.
Results may differ from a plain program's by a relative error of at most 0.009.
Values may be sent and summed in bfloat16 or wider, within the bound.
A program may use at most 32 MiB of HBM per device.

v0:
```python
import jax
import jax.numpy as jnp
from jax import lax
from jax.sharding import Mesh
from jax.sharding import PartitionSpec as P

D = 8192
FF = 26624
RANK = 256
FSDP = ("fsdp_0", "fsdp_1")
ROW = ("row_0", "row_1")
FSDP_ROW = ("fsdp_0", "fsdp_1", "row_0", "row_1")


def rows_for(lines, size):
    spare = -lines.shape[0] % size
    if not spare:
        return lines
    return jnp.concatenate([lines, jnp.zeros((spare, *lines.shape[1:]), lines.dtype)])


def own_block(blocks, axes, sequence):
    shape = [lax.axis_size(a) for a in axes]
    blocks = blocks.reshape(*shape, *blocks.shape[1:])
    blocks = blocks.transpose(*sequence, *range(len(axes), blocks.ndim))
    blocks = blocks.reshape(-1, *blocks.shape[len(axes) :])
    for k in sequence:
        blocks = lax.psum_scatter(blocks, axes[k], scatter_dimension=0, tiled=True)
    return blocks[0]


def gather_in_order(shard, axes, sequence):
    blocks = shard[None]
    for k in sequence:
        blocks = lax.all_gather(blocks, axes[k], axis=0, tiled=True)
    carried = [lax.axis_size(axes[k]) for k in reversed(sequence)]
    blocks = blocks.reshape(*carried, *shard.shape)
    turned = sorted(range(len(sequence)), key=lambda place: sequence[len(sequence) - 1 - place])
    return blocks.transpose(*turned, *range(len(sequence), blocks.ndim)).reshape(-1, *shard.shape)


def sum_at_once(shard, axes):
    size, count = (lax.axis_size(axes), len(axes))
    lines = shard.reshape(-1, *shard.shape[1:][-1:])
    blocks = rows_for(lines, size * count).reshape(count, size, -1, *lines.shape[1:])
    gathered = []
    for leading in range(count):
        sequence = [(leading + k) % count for k in range(count)]
        own = own_block(blocks[leading], axes, sequence)
        gathered.append(gather_in_order(own, axes, sequence[::-1]).reshape(-1, *lines.shape[1:]))
    return jnp.concatenate(gathered)[: len(lines)].reshape(shard.shape)


def over_pieces(shard, axis):
    blocks = lax.all_gather(shard, axis)
    return blocks.sum(axis=0)


def in_blocks(shard, dim, size):
    before, after = (shard.shape[:dim], shard.shape[dim + 1 :])
    return jnp.moveaxis(shard.reshape(*before, size, -1, *after), dim, 0)


def summed_on_arrival(shard, axis, dim):
    size = lax.axis_size(axis)
    blocks = lax.all_to_all(in_blocks(shard, dim, size), axis, 0, 0, tiled=True)
    return jnp.sum(blocks, axis=0)


def over_axes(shard, axes):
    for axis in axes:
        shard = lax.psum(shard, axis)
    return shard


def joined_along(blocks, dim):
    blocks = jnp.moveaxis(blocks, 0, dim)
    shape = blocks.shape
    return blocks.reshape(*shape[:dim], shape[dim] * shape[dim + 1], *shape[dim + 2 :])


def sent_to_all(shard, axis):
    copies = jnp.broadcast_to(shard, (lax.axis_size(axis), *shard.shape))
    return lax.all_to_all(copies, axis, split_axis=0, concat_axis=0, tiled=True)


def collect(shard, axis, dim):
    return joined_along(sent_to_all(shard, axis), dim)


def factor_rows(power, gram):
    lower = jnp.linalg.cholesky(gram)
    return lax.linalg.triangular_solve(
        lower, power, left_side=False, lower=True, transpose_a=True
    ).astype(jnp.bfloat16)


def gram_terms(power):
    return jnp.einsum("rk,rl->kl", power, power, preferred_element_type=jnp.float32)


def per_device(weight, momentum, gradient, basis):
    buffer = (momentum.astype(jnp.float32) + gradient.astype(jnp.float32)).astype(jnp.bfloat16)
    partial_power = jnp.dot(buffer, basis, preferred_element_type=jnp.float32)
    summed = sum_at_once(partial_power, FSDP)
    gram = over_pieces(gram_terms(summed), ROW)
    ortho = factor_rows(summed, gram)
    share = summed_on_arrival(
        jnp.einsum("rc,rk->ck", buffer, ortho, preferred_element_type=jnp.float32), ROW, 0
    )
    colsq = over_axes(jnp.sum(share * share, axis=0), FSDP_ROW)
    whole = collect(share.astype(jnp.bfloat16), ROW, 0)
    basis_new = (whole.astype(jnp.float32) / jnp.sqrt(colsq + 1e-06)).astype(jnp.bfloat16)
    feedback = jnp.einsum("rk,ck->rc", ortho, whole, preferred_element_type=jnp.float32)
    momentum_new = (buffer.astype(jnp.float32) - 0.5 * feedback).astype(jnp.bfloat16)
    coeff = 0.3 * (D * FF / RANK) ** 0.5 / 50.0
    update = jnp.einsum("rk,ck->rc", ortho, basis_new, preferred_element_type=jnp.float32)
    weight_new = (weight.astype(jnp.float32) - coeff * update).astype(jnp.bfloat16)
    return (weight_new, momentum_new, basis_new)


def solution(mesh):
    finer = Mesh(mesh.devices.reshape(16, 4, 8, 2), ("fsdp_0", "fsdp_1", "row_0", "row_1"))
    return jax.shard_map(
        per_device,
        mesh=finer,
        in_specs=(P(ROW, FSDP), P(ROW, FSDP), P(ROW, FSDP), P(FSDP, None)),
        out_specs=(P(ROW, FSDP), P(ROW, FSDP), P(FSDP, None)),
        check_vma=False,
    )
```

profile of v0, /device:TPU:1, one launch (start us, length us, event | category | flops | bytes accessed | tf_op | source)
XLA Modules:
  0.0 505.6 jit_solution(5443652910559440423)
XLA Ops:
  7.2 0.9 copy-done
  8.1 1.5 fusion.15
  9.7 0.9 copy.13
  10.7 0.8 reshape_reshape_squeeze.3
  11.4 38.7 %reduce-scatter.2.cloned.1.call-done = f32[16,4,256]{2,0,1:T(8,128)} async-done(((f32[64,4,256]{2,0,1:T(8,128)}), f32[16,4,256]{2,0,1:T(8,128)}) %reduce-scatter.2.cloned.1.call-update) | async-done | bytes 65552 | tf_op jit(solution)/shard_map/reduce_scatter | solution.py:28
  50.1 1.5 copy.14
  51.7 1.3 dynamic-slice.3
  53.0 1.3 dynamic-slice.5
  55.0 134.0 %all-reduce.7.cloned.1.call-done = (f32[64,4,256]{2,1,0:T(4,128)}, f32[16,4,256]{2,1,0:T(4,128)}) async-done(((f32[64,4,256]{2,1,0:T(4,128)}, f32[16,4,256]{2,1,0:T(4,128)}), (f32[64,4,256]{2,1,0:T(4,128)}, f32[16,4,256]{2,1,0:T(4,128)})) %all-reduce.7.cloned.1.call-update) | async-done | bytes 327696
  189.0 0.7 constant_dynamic-slice_fusion.3
  189.7 13.4 %all-reduce.2 = f32[4,4,256]{2,1,0:T(4,128)S(1)} all-reduce(f32[4,4,256]{2,1,0:T(4,128)S(1)} %constant_dynamic-slice_fusion.3), channel_id=4, replica_groups=mesh['fsdp_0'=16,'fsdp_1'=4,'row_0'=8,'row_1'=2] {'fsdp_1'}, use_global_device_ids=true, to_apply=%region_1.0.clone | all-reduce | flops 4096 | bytes 32768
  203.2 0.7 constant_dynamic-slice_fusion.2
  203.9 9.1 %all_gather.18 = f32[4,4,256]{2,1,0:T(4,128)S(1)} all-gather(f32[1,4,256]{2,1,0:T(4,128)S(1)} %constant_dynamic-slice_fusion.2), channel_id=1, replica_groups=mesh['fsdp_0'=16,'fsdp_1'=4,'row_0'=8,'row_1'=2] {'fsdp_1'}, dimensions={0}, use_global_device_ids=true | all-gather | bytes 20480 | tf_op jit(solution)/shard_map/all_gather | solution.py:35
  213.0 20.9 %all_gather.19 = f32[64,4,256]{2,1,0:T(4,128)S(1)} all-gather(f32[4,4,256]{2,1,0:T(4,128)S(1)} %all_gather.18), channel_id=1, replica_groups=mesh['fsdp_0'=16,'fsdp_1'=4,'row_0'=8,'row_1'=2] {'fsdp_0'}, dimensions={0}, use_global_device_ids=true | all-gather | bytes 278528 | tf_op jit(solution)/shard_map/all_gather | solution.py:35
  234.1 1.3 constant_dynamic-slice_fusion.1
  235.4 20.9 %all_gather.20 = f32[16,4,256]{2,1,0:T(4,128)S(1)} all-gather(f32[1,4,256]{2,1,0:T(4,128)S(1)} %constant_dynamic-slice_fusion.1), channel_id=1, replica_groups=mesh['fsdp_0'=16,'fsdp_1'=4,'row_0'=8,'row_1'=2] {'fsdp_0'}, dimensions={0}, use_global_device_ids=true | all-gather | bytes 69632 | tf_op jit(solution)/shard_map/all_gather | solution.py:35
  256.3 9.7 %all_gather.21 = f32[64,4,256]{2,0,1:T(8,128)S(1)} all-gather(f32[16,4,256]{2,0,1:T(8,128)S(1)} %copy.15), channel_id=1, replica_groups=mesh['fsdp_0'=16,'fsdp_1'=4,'row_0'=8,'row_1'=2] {'fsdp_1'}, dimensions={0}, use_global_device_ids=true | all-gather | bytes 327680 | tf_op jit(solution)/shard_map/all_gather | solution.py:35
  266.0 0.2 copy.16
  266.2 0.1 reshape_reshape.3
  266.3 1.0 fusion.19
  267.3 77.7 %all-gather.3.cloned.1.call-done = f32[4096,256]{1,0:T(8,128)} async-done(((f32[256,256]{1,0:T(8,128)}), f32[4096,256]{1,0:T(8,128)}) %all-gather.3.cloned.1.call-update) | async-done | bytes 4194320 | tf_op jit(solution)/shard_map/all_gather | solution.py:55
  345.0 2.5 reduce_sum.27
  347.6 0.1 copy.17
  347.8 11.7 %cholesky.50 = f32[128,128]{1,0:T(8,128)S(1)} custom-call(f32[128,128]{1,0:T(8,128)S(1)} %cholesky.118), custom_call_target="Cholesky" | custom-call | tf_op jit(solution)/shard_map/jit(cholesky)/cholesky | solution.py:92
  359.5 9.8 %custom-call.14 = f32[1,128,128]{1,2,0:T(8,128)S(1)} custom-call(f32[1,128,128]{2,1,0:T(8,128)S(1)} %get-tuple-element.28), custom_call_target="InvertDiagBlocksLowerTriangular" | custom-call | tf_op jit(solution)/shard_map/jit(cholesky)/cholesky | solution.py:92
  369.3 0.2 constant_dynamic-update-slice_fusion.3
  369.6 0.3 convolution_subtract_fusion.1
  369.8 11.7 %cholesky.105 = f32[128,128]{1,0:T(8,128)S(1)} custom-call(f32[128,128]{1,0:T(8,128)S(1)} %convolution_subtract_fusion.1), custom_call_target="Cholesky" | custom-call | tf_op jit(solution)/shard_map/jit(cholesky)/cholesky | solution.py:92
  381.6 0.6 compare_reduce_fusion
  383.6 4.1 while.1
  383.8 0.6 fusion.30
  384.4 1.4 bitcast_dynamic-update-slice_fusion.2
  385.8 0.6 fusion.30
  386.4 1.4 bitcast_dynamic-update-slice_fusion.2
  387.8 19.7 %custom-call.15 = f32[2,128,128]{1,2,0:T(8,128)S(1)} custom-call(f32[2,128,128]{2,1,0:T(8,128)S(1)} %get-tuple-element.10), custom_call_target="InvertDiagBlocksLowerTriangular" | custom-call | tf_op jit(solution)/shard_map/triangular_solve | solution.py:93
  407.4 0.4 fusion.18
  407.9 0.6 convolution_subtract_fusion
  408.5 0.4 convolution_convert_fusion
  408.9 0.3 fusion.7
  409.3 21.5 %all_to_all.10 = f32[16,26,256]{2,1,0:T(8,128)S(1)} all-to-all(f32[16,26,256]{2,1,0:T(8,128)S(1)} %reshape.43), channel_id=1, replica_groups=mesh['fsdp_0'=16,'fsdp_1'=4,'row_0'=8,'row_1'=2] {'row_0','row_1'}, dimensions={0} | all-to-all | bytes 851968 | tf_op jit(solution)/shard_map/all_to_all | solution.py:66
  430.9 0.7 broadcast_in_dim.6
  431.6 3.4 all-to-all-start.1
  435.0 25.9 %psum.28 = f32[256]{0:T(256)S(1)} all-reduce(f32[256]{0:T(256)S(1)} %get-tuple-element.29), channel_id=1, replica_groups=mesh['fsdp_0'=16,'fsdp_1'=4,'row_0'=8,'row_1'=2] {'fsdp_0'}, use_global_device_ids=true, to_apply=%region_11.12 | all-reduce | flops 256 | bytes 2048 | tf_op jit(solution)/shard_map/psum | solution.py:72
  461.0 8.4 %psum.29 = f32[256]{0:T(256)S(1)} all-reduce(f32[256]{0:T(256)S(1)} %psum.28), channel_id=1, replica_groups=mesh['fsdp_0'=16,'fsdp_1'=4,'row_0'=8,'row_1'=2] {'fsdp_1'}, use_global_device_ids=true, to_apply=%region_12.13 | all-reduce | flops 256 | bytes 2048 | tf_op jit(solution)/shard_map/psum | solution.py:72
  469.3 12.5 %psum.30 = f32[256]{0:T(256)S(1)} all-reduce(f32[256]{0:T(256)S(1)} %psum.29), channel_id=1, replica_groups=mesh['fsdp_0'=16,'fsdp_1'=4,'row_0'=8,'row_1'=2] {'row_0'}, use_global_device_ids=true, to_apply=%region_13.14 | all-reduce | flops 256 | bytes 2048 | tf_op jit(solution)/shard_map/psum | solution.py:72
  481.8 15.0 %psum.31 = f32[256]{0:T(256)S(1)} all-reduce(f32[256]{0:T(256)S(1)} %psum.30), channel_id=1, replica_groups=mesh['fsdp_0'=16,'fsdp_1'=4,'row_0'=8,'row_1'=2] {'row_1'}, use_global_device_ids=true, to_apply=%region_14.15 | all-reduce | flops 256 | bytes 2048 | tf_op jit(solution)/shard_map/psum | solution.py:72
  497.0 1.0 fusion.2
  498.1 1.0 fusion.3
  (39 shorter events, 0.9 us)
Async XLA Ops:
  7.2 0.9 copy-start
  7.2 42.9 %reduce-scatter.2.cloned.1.call-start = ((), (), s32[]{:S(2)}) async-start(), calls=%async_computation.3 | async-start | bytes 327680 | tf_op jit(solution)/shard_map/reduce_scatter | solution.py:28
  10.6 178.4 %all-reduce.7.cloned.1.call-start = ((), (), s32[]{:S(2)}) async-start(), calls=%async_computation.5 | async-start | bytes 655360
  51.6 293.4 %all-gather.3.cloned.1.call-start = ((), (), s32[]{:S(2)}) async-start(), calls=%async_computation.4 | async-start | bytes 4456448 | tf_op jit(solution)/shard_map/all_gather | solution.py:55
  345.0 63.9 %copy-start.1 = (bf16[512,416]{0,1:T(8,128)(2,1)S(1)}, bf16[512,416]{0,1:T(8,128)(2,1)}, u32[]{:S(2)}) copy-start(bf16[512,416]{0,1:T(8,128)(2,1)} %param.6) | copy-start | bytes 1277956
  345.0 63.9 %copy-start.2 = (bf16[512,416]{0,1:T(8,128)(2,1)S(1)}, bf16[512,416]{0,1:T(8,128)(2,1)}, u32[]{:S(2)}) copy-start(bf16[512,416]{0,1:T(8,128)(2,1)} %param.5) | copy-start | bytes 1277956
  408.5 89.6 %copy-start.4 = (bf16[512,416]{0,1:T(8,128)(2,1)S(1)}, bf16[512,416]{0,1:T(8,128)(2,1)}, u32[]{:S(2)}) copy-start(bf16[512,416]{0,1:T(8,128)(2,1)} %param.4) | copy-start | bytes 1277956
  431.6 65.3 %all-to-all-start.1 = ((bf16[16,26,256]{2,1,0:T(8,128)(2,1)}), bf16[16,26,256]{2,1,0:T(8,128)(2,1)S(1)}, u32[]{:S(2)}, u32[]{:S(2)}) async-start(bf16[16,26,256]{2,1,0:T(8,128)(2,1)} %broadcast_in_dim.6), calls=%async_computation.2 | async-start | bytes 524288 | tf_op jit(solution)/shard_map/all_to_all | solution.py:84
  498.1 1.0 copy-start.3
Sparse Core Ops, SparseCore 0:
  11.9 38.1 reduce-scatter.1
  53.1 135.8 all-reduce.6
  267.4 77.5 all-gather.2
where the time goes:
time: 506 us
  waiting for transfers between devices  250 us (49%)
  blocking collectives  157 us (31%)
  other arithmetic  56.4 us (11%)
  between operations  16 us (3%)
  local copies, waits for them, and re-layouts  15 us (3%)
  matrix products  6.73 us (1%)
    unnamed x4, waiting for transfers between devices  134 us
    all_gather x1, waiting for transfers between devices, over_pieces(): blocks = lax.all_gather(shard, axis)  77.7 us
    psum x4, blocking collectives, over_axes(): shard = lax.psum(shard, axis)  61.8 us
    all_gather x4, blocking collectives, gather_in_order(): blocks = lax.all_gather(blocks, axes[k], axis=0, tiled=True)  60.6 us
    reduce_scatter x1, waiting for transfers between devices, own_block(): blocks = lax.psum_scatter(blocks, axes[k], scatter_dimension=0, tiled=True)  38.7 us
    another operation x6, other arithmetic, factor_rows(): lower = jnp.linalg.cholesky(gram)  33.9 us
    all_to_all x1, blocking collectives, summed_on_arrival(): blocks = lax.all_to_all(in_blocks(shard, dim, size), axis, 0, 0, tiled=True)  21.5 us
    another operation x3, other arithmetic, factor_rows(): lax.linalg.triangular_solve(lower, power, left_side=False, lower=True, tr...  19.7 us
  transfers between devices with their start and end apart: 4, of which 3 were waited for; matrix products, arithmetic and copies ran while one was open for 1% of the time, Pallas kernels for 0%

commit v1 on v0

v1 whole, which is shorter than its diff:
```python
import functools

import jax
import jax.numpy as jnp
from jax import lax
from jax.experimental import pallas as pl
from jax.experimental.pallas import tpu as pltpu
from jax.sharding import Mesh
from jax.sharding import PartitionSpec as P

D = 8192
FF = 26624
RANK = 256
Z, X, Y, C = "fsdp_0", "fsdp_1", "row_0", "row_1"
FSDP = (Z, X)
ROW = (Y, C)
SIZES = (16, 4, 8, 2)
BF, F32 = jnp.bfloat16, jnp.float32
PAD = 512
MESH = pl.DeviceIdType.MESH


def far_first(n):
    return sorted(range(1, n), key=lambda d: -min(d, n - d))


def far_pairs(n, m):
    pairs = [(a, b) for a in range(n) for b in range(m) if a or b]
    return sorted(pairs, key=lambda p: -(min(p[0], n - p[0]) + min(p[1], m - p[1])))


def rows(start, size):
    return pl.ds(pl.multiple_of(start, size), size)


def wrap(i, n):
    return lax.rem(i, n)


def remote(src, dst, send, recv, peer):
    return pltpu.make_async_remote_copy(
        src_ref=src, dst_ref=dst, send_sem=send, recv_sem=recv, device_id=peer, device_id_type=MESH
    )


def power_kernel(
    sizes, m_ref, g_ref, b_ref, buft_ref, p_ref, gram_ref,
    wide, part, xbuf, zpart, zbuf, pbuf, gp, gbuf, gh, ybuf, gall,
    xs, xr, zs, zr, zs2, zr2, xs2, xr2, cs, cr, ys, yr, ys2, yr2, cs2, cr2,
):
    nz, nx, ny, nc = sizes
    z, x, y, c = (lax.axis_index(a) for a in (Z, X, Y, C))
    barrier = pltpu.get_barrier_semaphore()
    for axis, me, n in ((Z, z, nz), (X, x, nx), (Y, y, ny), (C, c, nc)):
        for d in far_first(n):
            pl.semaphore_signal(barrier, inc=1, device_id={axis: wrap(me + d, n)}, device_id_type=MESH)

    buffer = (m_ref[...].astype(F32) + g_ref[...].astype(F32)).astype(BF)
    part[...] = jnp.dot(buffer, b_ref[...], preferred_element_type=F32).astype(BF)
    pl.semaphore_wait(barrier, nz + nx + ny + nc - 4)

    nloc = part.shape[0]
    q = nloc // nx
    copies = []
    for d in far_first(nx):
        peer = wrap(x + d, nx)
        cp = remote(part.at[rows(peer * q, q)], xbuf.at[d], xs.at[d], xr.at[d], {X: peer})
        cp.start()
        copies.append(cp)
    wide[...] = jnp.zeros_like(wide)
    wide[:, : buffer.shape[1]] = buffer
    for cp in copies:
        cp.wait()
    total = part[rows(x * q, q), :].astype(F32)
    for d in range(1, nx):
        total += xbuf[d].astype(F32)
    zpart[...] = total.astype(BF)

    th = 2 * q // nz

    def tile(i):
        return (rows(lax.div(i, 2) * th, th), rows(lax.rem(i, 2) * 128, 128))

    copies = []
    for d in far_first(nz):
        peer = wrap(z + d, nz)
        cp = remote(zpart.at[tile(peer)], zbuf.at[d], zs.at[d], zr.at[d], {Z: peer})
        cp.start()
        copies.append(cp)
    buft_ref[...] = wide[...].T
    for cp in copies:
        cp.wait()
    own = zpart[tile(z)].astype(F32)
    for d in range(1, nz):
        own += zbuf[d].astype(F32)

    def ptile(i):
        return (rows(x * q + lax.div(i, 2) * th, th), rows(lax.rem(i, 2) * 128, 128))

    pbuf[ptile(z)] = own.astype(BF)
    copies = []
    for d in far_first(nz):
        cp = remote(pbuf.at[ptile(z)], pbuf.at[ptile(z)], zs2.at[d], zr2.at[d], {Z: wrap(z + d, nz)})
        cp.start()
        copies.append(cp)
    for d, cp in zip(far_first(nz), copies):
        cp.wait_send()
        src = wrap(z - d + nz, nz)
        remote(pbuf.at[ptile(src)], pbuf.at[ptile(src)], zs2.at[d], zr2.at[d], {Z: src}).wait_recv()

    mine = rows(x * q, q)
    copies = []
    for d in far_first(nx):
        cp = remote(pbuf.at[mine], pbuf.at[mine], xs2.at[d], xr2.at[d], {X: wrap(x + d, nx)})
        cp.start()
        copies.append(cp)
    gp[...] = gram_of(pbuf[mine, :])
    for d in sorted(range(1, nx), key=lambda d: min(d, nx - d)):
        src = wrap(x - d + nx, nx)
        there = rows(src * q, q)
        remote(pbuf.at[there], pbuf.at[there], xs2.at[d], xr2.at[d], {X: src}).wait_recv()
        gp[...] += gram_of(pbuf[there, :])
    for cp in copies:
        cp.wait_send()

    h = RANK // 2
    peer = {C: 1 - c}
    cp = remote(gp.at[rows((1 - c) * h, h)], gbuf, cs, cr, peer)
    cp.start()
    p_ref[...] = pbuf[...]
    cp.wait()
    gh[...] = gp[rows(c * h, h), :] + gbuf[...]

    s = h // ny
    copies = []
    for d in far_first(ny):
        to = wrap(y + d, ny)
        cp = remote(gh.at[rows(to * s, s)], ybuf.at[d], ys.at[d], yr.at[d], {Y: to})
        cp.start()
        copies.append(cp)
    for cp in copies:
        cp.wait()
    own = gh[rows(y * s, s), :]
    for d in range(1, ny):
        own += ybuf[d]

    def slot(i):
        return rows(c * h + i * s, s)

    gall[slot(y), :] = own
    copies = []
    for d in far_first(ny):
        cp = remote(gall.at[slot(y)], gall.at[slot(y)], ys2.at[d], yr2.at[d], {Y: wrap(y + d, ny)})
        cp.start()
        copies.append(cp)
    for d, cp in zip(far_first(ny), copies):
        cp.wait_send()
        src = wrap(y - d + ny, ny)
        remote(gall.at[slot(src)], gall.at[slot(src)], ys2.at[d], yr2.at[d], {Y: src}).wait_recv()
    half = rows(c * h, h)
    cp = remote(gall.at[half], gall.at[half], cs2, cr2, peer)
    cp.start()
    cp.wait_send()
    other = rows((1 - c) * h, h)
    remote(gall.at[other], gall.at[other], cs2, cr2, peer).wait_recv()
    gram_ref[...] = gall[...]


def gram_of(block):
    return lax.dot_general(block, block, (((0,), (0,)), ((), ())), preferred_element_type=F32)


def full(a, b, dims):
    return lax.dot_general(
        a, b, (dims, ((), ())), precision=lax.Precision.HIGHEST, preferred_element_type=F32
    )


def factor_kernel(g_ref, hi_ref, lo_ref, sym, low):
    n = RANK
    i = lax.broadcasted_iota(jnp.int32, (n, n), 0)
    j = lax.broadcasted_iota(jnp.int32, (n, n), 1)
    gram = g_ref[...]
    diag = jnp.where(i == j, gram, 0.0)
    across = lax.rsqrt(jnp.sum(diag, axis=0, keepdims=True))
    down = lax.rsqrt(jnp.sum(diag, axis=1, keepdims=True))
    sym[...] = gram * across * down
    eye = jnp.where(i == j, 1.0, 0.0)

    def phi(e):
        return jnp.where(i > j, e, jnp.where(i == j, 0.5 * e, 0.0))

    low[...] = eye - phi(sym[...] - eye)
    small = 1e-4

    def more(state):
        step, err = state
        return jnp.logical_and(step < 12, err > small)

    def newton(state):
        step, _ = state
        inv = low[...]
        e = full(full(inv, sym[...], ((1,), (0,))), inv, ((1,), (1,)))
        e = e - jnp.where(i == j, 1.0, 0.0)
        low[...] = inv - full(phi(e), inv, ((1,), (0,)))
        return step + 1, jnp.sum(e * e)

    _, err = lax.while_loop(more, newton, (0, jnp.float32(1.0)))

    @pl.when(jnp.logical_not(err <= small))
    def _():
        sym[...] = g_ref[...] * across * down
        low[...] = jnp.where(i == j, 1.0, 0.0)
        lane = lax.broadcasted_iota(jnp.int32, (1, n), 1)
        line = lax.broadcasted_iota(jnp.int32, (n, 1), 0)

        def column(k, _):
            pivots = sym[pl.ds(k, 1), :]
            pivot = jnp.sum(jnp.where(lane == k, pivots, 0.0), axis=1, keepdims=True)
            inverse = low[pl.ds(k, 1), :]
            here = sym[...]
            col = jnp.sum(jnp.where(j == k, here, 0.0), axis=1, keepdims=True)
            times = jnp.where(line > k, col / pivot, 0.0)
            sym[...] = here - times * pivots
            low[...] = low[...] - times * inverse
            return 0

        lax.fori_loop(0, n, column, 0)
        pivot = jnp.sum(jnp.where(i == j, sym[...], 0.0), axis=1, keepdims=True)
        low[...] = low[...] * lax.rsqrt(pivot)

    inv = low[...] * across
    hi = inv.astype(BF)
    hi_ref[...] = hi
    lo_ref[...] = (inv - hi.astype(F32)).astype(BF)


def right_kernel(
    sizes, p_ref, hi_ref, lo_ref, buft_ref, ortho_ref, right_ref, colsq_ref,
    part, cbuf, half, ybuf, rall, sq1, sq2,
    cs, cr, ys, yr, ys2, yr2, cs2, cr2, s1, r1, s2, r2,
):
    nz, nx, ny, nc = sizes
    z, x, y, c = (lax.axis_index(a) for a in (Z, X, Y, C))
    barrier = pltpu.get_barrier_semaphore()
    plane = far_pairs(ny, nx)
    line = far_pairs(nz, nc)
    for dz, dc in line:
        to = {Z: wrap(z + dz, nz), C: wrap(c + dc, nc)}
        pl.semaphore_signal(barrier, inc=1, device_id=to, device_id_type=MESH)
    for dy, dx in plane:
        to = {Y: wrap(y + dy, ny), X: wrap(x + dx, nx)}
        pl.semaphore_signal(barrier, inc=1, device_id=to, device_id_type=MESH)

    across = (((1,), (1,)), ((), ()))
    power = p_ref[...]
    ortho = lax.dot_general(power, hi_ref[...], across, preferred_element_type=F32)
    ortho += lax.dot_general(power, lo_ref[...], across, preferred_element_type=F32)
    ortho = ortho.astype(BF)
    ortho_ref[...] = ortho
    part[...] = jnp.dot(buft_ref[...], ortho, preferred_element_type=F32).astype(BF)
    pl.semaphore_wait(barrier, len(plane) + len(line))

    h = PAD // 2
    peer = {C: 1 - c}
    cp = remote(part.at[rows((1 - c) * h, h)], cbuf, cs, cr, peer)
    cp.start()
    cp.wait()
    half[...] = (part[rows(c * h, h), :].astype(F32) + cbuf[...].astype(F32)).astype(BF)

    s = h // ny
    copies = []
    for d in far_first(ny):
        to = wrap(y + d, ny)
        cp = remote(half.at[rows(to * s, s)], ybuf.at[d], ys.at[d], yr.at[d], {Y: to})
        cp.start()
        copies.append(cp)
    for cp in copies:
        cp.wait()
    own = half[rows(y * s, s), :].astype(F32)
    for d in range(1, ny):
        own += ybuf[d].astype(F32)

    sq1[0] = jnp.sum(own * own, axis=0, keepdims=True)
    first = []
    for dy, dx in plane:
        k = dy * nx + dx
        to = {Y: wrap(y + dy, ny), X: wrap(x + dx, nx)}
        cp = remote(sq1.at[0], sq1.at[k], s1.at[k], r1.at[k], to)
        cp.start()
        first.append(cp)

    def slot(i):
        return rows(c * h + i * s, s)

    rall[slot(y), :] = own.astype(BF)
    gather = []
    for d in far_first(ny):
        cp = remote(rall.at[slot(y)], rall.at[slot(y)], ys2.at[d], yr2.at[d], {Y: wrap(y + d, ny)})
        cp.start()
        gather.append(cp)

    for cp in first:
        cp.wait()
    sq2[0] = jnp.sum(sq1[...], axis=0)
    second = []
    for dz, dc in line:
        k = dz * nc + dc
        to = {Z: wrap(z + dz, nz), C: wrap(c + dc, nc)}
        cp = remote(sq2.at[0], sq2.at[k], s2.at[k], r2.at[k], to)
        cp.start()
        second.append(cp)

    for d, cp in zip(far_first(ny), gather):
        cp.wait_send()
        src = wrap(y - d + ny, ny)
        remote(rall.at[slot(src)], rall.at[slot(src)], ys2.at[d], yr2.at[d], {Y: src}).wait_recv()
    mine = rows(c * h, h)
    cp = remote(rall.at[mine], rall.at[mine], cs2, cr2, peer)
    cp.start()
    cp.wait_send()
    other = rows((1 - c) * h, h)
    remote(rall.at[other], rall.at[other], cs2, cr2, peer).wait_recv()
    right_ref[...] = rall[...]
    for cp in second:
        cp.wait()
    colsq_ref[...] = jnp.sum(sq2[...], axis=0)


def vmem(n):
    return [pl.BlockSpec(memory_space=pltpu.VMEM)] * n


def per_device(sizes, weight, momentum, gradient, basis):
    nz, nx, ny, nc = sizes
    nloc, cols = momentum.shape
    q = nloc // nx
    th = 2 * q // nz
    h = RANK // 2
    dma = pltpu.SemaphoreType.DMA
    buft, power, gram = pl.pallas_call(
        functools.partial(power_kernel, sizes),
        out_shape=(
            jax.ShapeDtypeStruct((PAD, nloc), BF),
            jax.ShapeDtypeStruct((nloc, RANK), BF),
            jax.ShapeDtypeStruct((RANK, RANK), F32),
        ),
        in_specs=vmem(3),
        out_specs=tuple(vmem(3)),
        scratch_shapes=[
            pltpu.VMEM((nloc, PAD), BF),
            pltpu.VMEM((nloc, RANK), BF),
            pltpu.VMEM((nx, q, RANK), BF),
            pltpu.VMEM((q, RANK), BF),
            pltpu.VMEM((nz, th, 128), BF),
            pltpu.VMEM((nloc, RANK), BF),
            pltpu.VMEM((RANK, RANK), F32),
            pltpu.VMEM((h, RANK), F32),
            pltpu.VMEM((h, RANK), F32),
            pltpu.VMEM((ny, h // ny, RANK), F32),
            pltpu.VMEM((RANK, RANK), F32),
            dma((nx,)), dma((nx,)), dma((nz,)), dma((nz,)), dma((nz,)), dma((nz,)), dma((nx,)), dma((nx,)),
            dma, dma, dma((ny,)), dma((ny,)), dma((ny,)), dma((ny,)), dma, dma,
        ],
        compiler_params=pltpu.CompilerParams(collective_id=0, has_side_effects=True),
    )(momentum, gradient, basis)

    hi, lo = pl.pallas_call(
        factor_kernel,
        out_shape=(jax.ShapeDtypeStruct((RANK, RANK), BF),) * 2,
        in_specs=vmem(1),
        out_specs=tuple(vmem(2)),
        scratch_shapes=[pltpu.VMEM((RANK, RANK), F32)] * 2,
    )(gram)

    s = PAD // 2 // ny
    ortho, right, colsq = pl.pallas_call(
        functools.partial(right_kernel, sizes),
        out_shape=(
            jax.ShapeDtypeStruct((nloc, RANK), BF),
            jax.ShapeDtypeStruct((PAD, RANK), BF),
            jax.ShapeDtypeStruct((1, RANK), F32),
        ),
        in_specs=vmem(4),
        out_specs=tuple(vmem(3)),
        scratch_shapes=[
            pltpu.VMEM((PAD, RANK), BF),
            pltpu.VMEM((PAD // 2, RANK), BF),
            pltpu.VMEM((PAD // 2, RANK), BF),
            pltpu.VMEM((ny, s, RANK), BF),
            pltpu.VMEM((PAD, RANK), BF),
            pltpu.VMEM((ny * nx, 1, RANK), F32),
            pltpu.VMEM((nz * nc, 1, RANK), F32),
            dma, dma, dma((ny,)), dma((ny,)), dma((ny,)), dma((ny,)), dma, dma,
            dma((ny * nx,)), dma((ny * nx,)), dma((nz * nc,)), dma((nz * nc,)),
        ],
        compiler_params=pltpu.CompilerParams(collective_id=1, has_side_effects=True),
    )(power, hi, lo, buft)

    whole = right[:cols]
    buffer = (momentum.astype(F32) + gradient.astype(F32)).astype(BF)
    basis_new = (whole.astype(F32) / jnp.sqrt(colsq + 1e-06)).astype(BF)
    feedback = jnp.einsum("rk,ck->rc", ortho, whole, preferred_element_type=F32)
    momentum_new = (buffer.astype(F32) - 0.5 * feedback).astype(BF)
    coeff = 0.3 * (D * FF / RANK) ** 0.5 / 50.0
    update = jnp.einsum("rk,ck->rc", ortho, basis_new, preferred_element_type=F32)
    weight_new = (weight.astype(F32) - coeff * update).astype(BF)
    return (weight_new, momentum_new, basis_new)


def build(devices, sizes):
    finer = Mesh(devices.reshape(sizes), (Z, X, Y, C))
    return jax.shard_map(
        functools.partial(per_device, sizes),
        mesh=finer,
        in_specs=(P(ROW, FSDP), P(ROW, FSDP), P(ROW, FSDP), P(FSDP, None)),
        out_specs=(P(ROW, FSDP), P(ROW, FSDP), P(FSDP, None)),
        check_vma=False,
    )


def solution(mesh):
    return build(mesh.devices, SIZES)
```

time: 506 us -> 147 us (0.29)
  waiting for transfers between devices: 250 us -> 0 us
  blocking collectives: 157 us -> 0 us
  Pallas kernels: 0 us -> 138 us
  other arithmetic: 56.4 us -> 1.7 us
  between operations: 16 us -> 0.71 us
  local copies, waits for them, and re-layouts: 15 us -> 3.1 us
    pallas_call x0 -> x3, Pallas kernels: none -> 138 us  [the longest x1 63.4 us: per_device(): pl.pallas_call(functools.partial(power_kernel, sizes), out_shape=(jax.Sha...]
    unnamed x4 -> x0, waiting for transfers between devices: 134 us -> none
    all_gather x1 -> x0, waiting for transfers between devices: 77.7 us -> none  [over_pieces(): blocks = lax.all_gather(shard, axis)]
    psum x4 -> x0, blocking collectives: 61.8 us -> none  [over_axes(): shard = lax.psum(shard, axis)]
    all_gather x4 -> x0, blocking collectives: 60.6 us -> none  [gather_in_order(): blocks = lax.all_gather(blocks, axes[k], axis=0, tiled=True)]
    another operation x9 -> x0, other arithmetic: 53.7 us -> none  [the longest x6 33.9 us: factor_rows(): lower = jnp.linalg.cholesky(gram)]
    reduce_scatter x1 -> x0, waiting for transfers between devices: 38.7 us -> none  [own_block(): blocks = lax.psum_scatter(blocks, axes[k], scatter_dimension=0, tiled=True)]
    all_to_all x1 -> x0, blocking collectives: 21.5 us -> none  [summed_on_arrival(): blocks = lax.all_to_all(in_blocks(shard, dim, size), axis, 0, 0, tiled=True)]
  transfers between devices with their start and end apart: 4 -> 0, of which waited for: 3 -> 0; matrix products, arithmetic and copies ran while one was open for 1% -> 0% of each run, Pallas kernels for 0% -> 0%
where the time goes in v1:
time: 147 us
  Pallas kernels  138 us (94%)
  matrix products  3.24 us (2%)
  local copies, waits for them, and re-layouts  3.1 us (2%)
  other arithmetic  1.7 us (1%)
    pallas_call x1, Pallas kernels, per_device(): pl.pallas_call(functools.partial(power_kernel, sizes), out_shape=(jax.Sha...  63.4 us
    pallas_call x1, Pallas kernels, per_device(): pl.pallas_call(factor_kernel, out_shape=(jax.ShapeDtypeStruct((RANK, RANK...  44.3 us
    pallas_call x1, Pallas kernels, per_device(): pl.pallas_call(functools.partial(right_kernel, sizes), out_shape=(jax.Sha...  30.1 us
    unnamed x12, local copies, waits for them, and re-layouts  3.1 us

profile of v1, /device:TPU:1, one launch (start us, length us, event | category | flops | bytes accessed | tf_op | source)
XLA Modules:
  0.0 146.5 jit_solution(14980380028205885960)
XLA Ops:
  0.6 0.0 copy-start.1
  0.6 2.1 %copy.7.m_ref = bf16[512,416]{1,0:T(8,128)(2,1)} copy(bf16[512,416]{0,1:T(8,128)(2,1)} %param.5) | data formatting | bytes 851968 | tf_op args[1]
  2.7 0.0 copy-done.1
  2.7 1.0 copy.8.g_ref
  3.7 63.4 %shard_map.67 = (bf16[512,512]{1,0:T(8,128)(2,1)}, bf16[512,256]{1,0:T(8,128)(2,1)}, f32[256,256]{1,0:T(8,128)}) custom-call(bf16[512,416]{1,0:T(8,128)(2,1)} %copy.7.m_ref, bf16[512,416]{1,0:T(8,128)(2,1)} %copy.8.g_ref, bf16[416,256]{1,0:T(8,128)(2,1)} %b_ref.1), custom_call_target="tpu_custom_call" | custom-call | tf_op jit(solution)/shard_map/pallas_call | solution.py:341
  67.1 44.3 %shard_map.68 = (bf16[256,256]{1,0:T(8,128)(2,1)}, bf16[256,256]{1,0:T(8,128)(2,1)}) custom-call(f32[256,256]{1,0:T(8,128)} %get-tuple-element.12.g_ref), custom_call_target="tpu_custom_call" | custom-call | tf_op jit(solution)/shard_map/pallas_call | solution.py:368
  111.4 30.1 %shard_map.69 = (bf16[512,256]{1,0:T(8,128)(2,1)}, bf16[512,256]{1,0:T(8,128)(2,1)}, f32[1,256]{1,0:T(1,128)}) custom-call(bf16[512,256]{1,0:T(8,128)(2,1)} %get-tuple-element.11.p_ref, bf16[256,256]{1,0:T(8,128)(2,1)} %get-tuple-element.13.hi_ref, bf16[256,256]{1,0:T(8,128)(2,1)} %get-tuple-element.14.lo_ref, bf16[512,512]{1,0:T(8,128)(2,1)} %get-tuple-element.15.buft_ref), custom_call_target="tpu_custom_call" | custom-call | tf_op jit(solution)/shard_map/pallas_call | solution.py:377
  141.5 0.0 copy-start
  141.6 0.7 add_sqrt_fusion
  142.3 1.0 divide_convert_fusion
  143.3 0.0 copy-done
  143.3 0.0 copy-start.3
  143.3 0.0 copy-start.2
  143.3 0.0 copy-start.4
  143.3 2.2 %fusion.2 = bf16[512,416]{0,1:T(8,128)(2,1)} fusion(bf16[512,256]{1,0:T(8,128)(2,1)} %get-tuple-element.16, bf16[512,416]{0,1:T(8,128)(2,1)S(1)} %copy-done.1, bf16[512,416]{0,1:T(8,128)(2,1)S(1)} %copy-done, bf16[512,256]{1,0:T(8,128)(2,1)} %get-tuple-element.17), kind=kOutput, calls=%fused_computation.4 | convolution fusion | flops 110755840 | bytes 1753088 | tf_op jit(solution)/shard_map/rk,ck->rc/dot_general | solution.py:403
  145.5 0.0 copy-done.3
  145.5 0.0 copy-done.2
  145.5 0.0 copy-done.4
  145.5 1.1 fusion.3
Async XLA Ops:
  0.6 2.1 %copy-start.1 = (bf16[512,416]{0,1:T(8,128)(2,1)S(1)}, bf16[512,416]{0,1:T(8,128)(2,1)}, u32[]{:S(2)}) copy-start(bf16[512,416]{0,1:T(8,128)(2,1)} %param.6) | copy-start | bytes 1277956
  141.5 1.7 %copy-start = (bf16[512,416]{0,1:T(8,128)(2,1)S(1)}, bf16[512,416]{0,1:T(8,128)(2,1)}, u32[]{:S(2)}) copy-start(bf16[512,416]{0,1:T(8,128)(2,1)} %param.5) | copy-start | bytes 1277956
  143.3 2.2 %copy-start.3 = (bf16[416,256]{1,0:T(8,128)(2,1)}, bf16[416,256]{1,0:T(8,128)(2,1)S(1)}, u32[]{:S(2)}) copy-start(bf16[416,256]{1,0:T(8,128)(2,1)S(1)} %divide_convert_fusion) | copy-start | bytes 638980
  143.3 2.2 %copy-start.2 = (bf16[512,256]{1,0:T(8,128)(2,1)S(1)}, bf16[512,256]{1,0:T(8,128)(2,1)}, u32[]{:S(2)}) copy-start(bf16[512,256]{1,0:T(8,128)(2,1)} %get-tuple-element.16) | copy-start | bytes 786436
  143.3 2.2 %copy-start.4 = (bf16[512,416]{0,1:T(8,128)(2,1)S(1)}, bf16[512,416]{0,1:T(8,128)(2,1)}, u32[]{:S(2)}) copy-start(bf16[512,416]{0,1:T(8,128)(2,1)} %param.4) | copy-start | bytes 1277956

commit v2 on v1

v2 whole, which is shorter than its diff:
```python
import functools

import jax
import jax.numpy as jnp
from jax import lax
from jax.experimental import pallas as pl
from jax.experimental.pallas import tpu as pltpu
from jax.sharding import Mesh
from jax.sharding import PartitionSpec as P

D = 8192
FF = 26624
RANK = 256
Z, X, Y, C = "fsdp_0", "fsdp_1", "row_0", "row_1"
FSDP = (Z, X)
ROW = (Y, C)
SIZES = (16, 4, 8, 2)
BF, F32 = jnp.bfloat16, jnp.float32
PAD = 512
MESH = pl.DeviceIdType.MESH


def far_first(n):
    return sorted(range(1, n), key=lambda d: -min(d, n - d))


def far_pairs(n, m):
    pairs = [(a, b) for a in range(n) for b in range(m) if a or b]
    return sorted(pairs, key=lambda p: -(min(p[0], n - p[0]) + min(p[1], m - p[1])))


def rows(start, size):
    return pl.ds(pl.multiple_of(start, size), size)


def wrap(i, n):
    return lax.rem(i, n)


def near_first(n):
    return far_first(n)[::-1]


def remote(src, dst, send, recv, peer):
    return pltpu.make_async_remote_copy(
        src_ref=src, dst_ref=dst, send_sem=send, recv_sem=recv, device_id=peer, device_id_type=MESH
    )


def power_kernel(
    sizes, m_ref, g_ref, b_ref, buft_ref, p_ref, gram_ref,
    mv, gv, bv, part, xbuf, zpart, zbuf, pbuf, gp, gbuf, gh, ybuf, gall,
    ins, xs, xr, zs, zr, zs2, zr2, xs2, xr2, cs, cr, ys, yr, ys2, yr2, cs2, cr2,
):
    nz, nx, ny, nc = sizes
    z, x, y, c = (lax.axis_index(a) for a in (Z, X, Y, C))
    loads = [pltpu.make_async_copy(a, b, ins.at[i]) for i, (a, b) in enumerate(((m_ref, mv), (g_ref, gv), (b_ref, bv)))]
    for cp in loads:
        cp.start()
    barrier = pltpu.get_barrier_semaphore()
    for axis, me, n in ((Z, z, nz), (X, x, nx), (Y, y, ny), (C, c, nc)):
        for d in far_first(n):
            pl.semaphore_signal(barrier, inc=1, device_id={axis: wrap(me + d, n)}, device_id_type=MESH)
    for cp in loads:
        cp.wait()

    buffer = (mv[...].astype(F32) + gv[...].astype(F32)).astype(BF)
    buft_ref[...] = buffer
    part[...] = lax.dot_general(
        bv[...], buffer, (((0,), (0,)), ((), ())), preferred_element_type=F32
    ).astype(BF)
    pl.semaphore_wait(barrier, nz + nx + ny + nc - 4)

    q = part.shape[1] // nx
    th = RANK // nz
    order = far_first(nz) + [0]

    def tile(i, j):
        return (rows(i * th, th), rows(j * q, q))

    scatter = {}
    for e in order:
        to = wrap(z + e, nz)
        for d in far_first(nx):
            peer = wrap(x + d, nx)
            k = e * nx + d
            cp = remote(part.at[tile(to, peer)], xbuf.at[k], xs.at[k], xr.at[k], {X: peer})
            cp.start()
            scatter[k] = cp

    second = {}
    for e in order:
        to = wrap(z + e, nz)
        total = part[tile(to, x)].astype(F32)
        for d in far_first(nx):
            scatter[e * nx + d].wait_recv()
            total += xbuf[e * nx + d].astype(F32)
        if e:
            zpart[e] = total.astype(BF)
            second[e] = remote(zpart.at[e], zbuf.at[e], zs.at[e], zr.at[e], {Z: to})
            second[e].start()
        else:
            own = total
    for e in near_first(nz):
        second[e].wait_recv()
        own += zbuf[e].astype(F32)

    def forward(i):
        t = pbuf.at[tile(i, x)]
        for d in far_first(nx):
            remote(t, t, xs2.at[d], xr2.at[d], {X: wrap(x + d, nx)}).start()

    pbuf[tile(z, x)] = own.astype(BF)
    home = pbuf.at[tile(z, x)]
    gather = []
    for d in far_first(nz):
        cp = remote(home, home, zs2.at[d], zr2.at[d], {Z: wrap(z + d, nz)})
        cp.start()
        gather.append(cp)
    forward(z)
    for cp in list(scatter.values()) + list(second.values()):
        cp.wait_send()
    for d in near_first(nz):
        src = wrap(z - d + nz, nz)
        there = pbuf.at[tile(src, x)]
        remote(there, there, zs2.at[d], zr2.at[d], {Z: src}).wait_recv()
        forward(src)
    for cp in gather:
        cp.wait_send()

    def quarter(j):
        return (pl.ds(0, RANK), rows(j * q, q))

    gp[...] = gram_of(pbuf[quarter(x)])
    for d in near_first(nx):
        src = wrap(x - d + nx, nx)
        there = pbuf.at[quarter(src)]
        remote(there, there, xs2.at[d], xr2.at[d], {X: src}).wait_recv()
        gp[...] += gram_of(pbuf[quarter(src)])

    h = RANK // 2
    peer = {C: 1 - c}
    cp = remote(gp.at[rows((1 - c) * h, h)], gbuf, cs, cr, peer)
    cp.start()
    for d in far_first(nx):
        mine = pbuf.at[quarter(x)]
        remote(mine, mine, xs2.at[d], xr2.at[d], {X: wrap(x + d, nx)}).wait_send()
    p_ref[...] = pbuf[...]
    cp.wait()
    gh[...] = gp[rows(c * h, h), :] + gbuf[...]

    s = h // ny
    copies = []
    for d in far_first(ny):
        to = wrap(y + d, ny)
        cp = remote(gh.at[rows(to * s, s)], ybuf.at[d], ys.at[d], yr.at[d], {Y: to})
        cp.start()
        copies.append(cp)
    for cp in copies:
        cp.wait()
    own = gh[rows(y * s, s), :]
    for d in range(1, ny):
        own += ybuf[d]

    def slot(i):
        return rows(c * h + i * s, s)

    def across(i):
        t = gall.at[slot(i)]
        remote(t, t, cs2, cr2, peer).start()

    gall[slot(y), :] = own
    copies = []
    for d in far_first(ny):
        cp = remote(gall.at[slot(y)], gall.at[slot(y)], ys2.at[d], yr2.at[d], {Y: wrap(y + d, ny)})
        cp.start()
        copies.append(cp)
    across(y)
    for d in near_first(ny):
        src = wrap(y - d + ny, ny)
        remote(gall.at[slot(src)], gall.at[slot(src)], ys2.at[d], yr2.at[d], {Y: src}).wait_recv()
        across(src)
    for cp in copies:
        cp.wait_send()
    half = rows(c * h, h)
    remote(gall.at[half], gall.at[half], cs2, cr2, peer).wait_send()
    other = rows((1 - c) * h, h)
    remote(gall.at[other], gall.at[other], cs2, cr2, peer).wait_recv()
    gram_ref[...] = gall[...]


def gram_of(block):
    return lax.dot_general(block, block, (((1,), (1,)), ((), ())), preferred_element_type=F32)


def full(a, b, dims):
    return lax.dot_general(
        a, b, (dims, ((), ())), precision=lax.Precision.HIGHEST, preferred_element_type=F32
    )


def quick(a, b, dims):
    return lax.dot_general(a.astype(BF), b.astype(BF), (dims, ((), ())), preferred_element_type=F32)


def newton_step(product, sym, low):
    n = RANK
    i = lax.broadcasted_iota(jnp.int32, (n, n), 0)
    j = lax.broadcasted_iota(jnp.int32, (n, n), 1)
    inv = low[...]
    e = product(product(inv, sym[...], ((1,), (0,))), inv, ((1,), (1,)))
    e = e - jnp.where(i == j, 1.0, 0.0)
    phi = jnp.where(i > j, e, jnp.where(i == j, 0.5 * e, 0.0))
    low[...] = inv - product(phi, inv, ((1,), (0,)))
    return jnp.sum(e * e)


def factor_kernel(g_ref, sym, low, scale_ref, work):
    n = RANK
    i = lax.broadcasted_iota(jnp.int32, (n, n), 0)
    j = lax.broadcasted_iota(jnp.int32, (n, n), 1)
    gram = g_ref[...]
    diag = jnp.where(i == j, gram, 0.0)
    across = lax.rsqrt(jnp.sum(diag, axis=0, keepdims=True))
    down = lax.rsqrt(jnp.sum(diag, axis=1, keepdims=True))
    scale_ref[...] = across
    normed = gram * across * down
    sym[...] = normed
    low[...] = jnp.where(i > j, -normed, jnp.where(i == j, 1.5 - 0.5 * normed, 0.0))
    small = 1e-2

    def more(state):
        step, err = state
        return jnp.logical_and(step < 12, err > small)

    def newton(state):
        return state[0] + 1, newton_step(quick, sym, low)

    _, err = lax.while_loop(more, newton, (0, jnp.float32(1.0)))

    @pl.when(jnp.logical_not(err <= small))
    def _():
        work[...] = sym[...]
        low[...] = jnp.where(i == j, 1.0, 0.0)
        lane = lax.broadcasted_iota(jnp.int32, (1, n), 1)
        line = lax.broadcasted_iota(jnp.int32, (n, 1), 0)

        def column(k, _):
            pivots = work[pl.ds(k, 1), :]
            pivot = jnp.sum(jnp.where(lane == k, pivots, 0.0), axis=1, keepdims=True)
            inverse = low[pl.ds(k, 1), :]
            here = work[...]
            col = jnp.sum(jnp.where(j == k, here, 0.0), axis=1, keepdims=True)
            times = jnp.where(line > k, col / pivot, 0.0)
            work[...] = here - times * pivots
            low[...] = low[...] - times * inverse
            return 0

        lax.fori_loop(0, n, column, 0)
        pivot = jnp.sum(jnp.where(i == j, work[...], 0.0), axis=1, keepdims=True)
        low[...] = low[...] * lax.rsqrt(pivot)


def right_kernel(
    sizes, p_ref, sym, low_ref, scale_ref, buft_ref, w_ref,
    ortho_ref, right_ref, colsq_ref, mom_ref, wout_ref,
    low, part, cbuf, half, ybuf, rall, sq1, sq2,
    ins, cs, cr, ys, yr, ys2, yr2, cs2, cr2, s1, r1, s2, r2,
):
    nz, nx, ny, nc = sizes
    z, x, y, c = (lax.axis_index(a) for a in (Z, X, Y, C))
    barrier = pltpu.get_barrier_semaphore()
    plane = far_pairs(ny, nx)
    line = far_pairs(nz, nc)
    for dz, dc in line:
        to = {Z: wrap(z + dz, nz), C: wrap(c + dc, nc)}
        pl.semaphore_signal(barrier, inc=1, device_id=to, device_id_type=MESH)
    for dy, dx in plane:
        to = {Y: wrap(y + dy, ny), X: wrap(x + dx, nx)}
        pl.semaphore_signal(barrier, inc=1, device_id=to, device_id_type=MESH)
    load = pltpu.make_async_copy(w_ref, wout_ref, ins)
    load.start()

    low[...] = low_ref[...]
    for _ in range(2):
        newton_step(full, sym, low)
    inv = low[...] * scale_ref[...]
    hi = inv.astype(BF)
    lo = (inv - hi.astype(F32)).astype(BF)
    power = p_ref[...]
    ortho = jnp.dot(hi, power, preferred_element_type=F32)
    ortho += jnp.dot(lo, power, preferred_element_type=F32)
    ortho = ortho.astype(BF)
    ortho_ref[...] = ortho
    cols = buft_ref.shape[0]
    part[:cols, :] = lax.dot_general(
        buft_ref[...], ortho, (((1,), (1,)), ((), ())), preferred_element_type=F32
    ).astype(BF)
    part[cols:, :] = jnp.zeros((PAD - cols, RANK), BF)
    pl.semaphore_wait(barrier, len(plane) + len(line))

    h = PAD // 2
    peer = {C: 1 - c}
    cp = remote(part.at[rows((1 - c) * h, h)], cbuf, cs, cr, peer)
    cp.start()
    cp.wait()
    half[...] = (part[rows(c * h, h), :].astype(F32) + cbuf[...].astype(F32)).astype(BF)

    s = h // ny
    copies = []
    for d in far_first(ny):
        to = wrap(y + d, ny)
        cp = remote(half.at[rows(to * s, s)], ybuf.at[d], ys.at[d], yr.at[d], {Y: to})
        cp.start()
        copies.append(cp)
    for cp in copies:
        cp.wait()
    own = half[rows(y * s, s), :].astype(F32)
    for d in range(1, ny):
        own += ybuf[d].astype(F32)

    sq1[0] = jnp.sum(own * own, axis=0, keepdims=True)
    first = []
    for dy, dx in plane:
        k = dy * nx + dx
        to = {Y: wrap(y + dy, ny), X: wrap(x + dx, nx)}
        cp = remote(sq1.at[0], sq1.at[k], s1.at[k], r1.at[k], to)
        cp.start()
        first.append(cp)

    def slot(i):
        return rows(c * h + i * s, s)

    rall[slot(y), :] = own.astype(BF)
    gather = []
    for d in far_first(ny):
        cp = remote(rall.at[slot(y)], rall.at[slot(y)], ys2.at[d], yr2.at[d], {Y: wrap(y + d, ny)})
        cp.start()
        gather.append(cp)

    for cp in first:
        cp.wait()
    sq2[0] = jnp.sum(sq1[...], axis=0)
    second = []
    for dz, dc in line:
        k = dz * nc + dc
        to = {Z: wrap(z + dz, nz), C: wrap(c + dc, nc)}
        cp = remote(sq2.at[0], sq2.at[k], s2.at[k], r2.at[k], to)
        cp.start()
        second.append(cp)

    for d, cp in zip(far_first(ny), gather):
        cp.wait_send()
        src = wrap(y - d + ny, ny)
        remote(rall.at[slot(src)], rall.at[slot(src)], ys2.at[d], yr2.at[d], {Y: src}).wait_recv()
    mine = rows(c * h, h)
    cp = remote(rall.at[mine], rall.at[mine], cs2, cr2, peer)
    cp.start()
    cp.wait_send()
    other = rows((1 - c) * h, h)
    remote(rall.at[other], rall.at[other], cs2, cr2, peer).wait_recv()
    right_ref[...] = rall[...]
    feedback = jnp.dot(rall[:cols, :], ortho_ref[...], preferred_element_type=F32)
    mom_ref[...] = (buft_ref[...].astype(F32) - 0.5 * feedback).astype(BF)
    load.wait()
    for cp in second:
        cp.wait()
    colsq_ref[...] = jnp.sum(sq2[...], axis=0)


def update_kernel(
    ortho_ref, right_ref, colsq_ref, mom_ref, w_ref, weight_ref, momentum_ref, basis_ref, wv, bv, outs
):
    first = pltpu.make_async_copy(mom_ref, momentum_ref, outs.at[0])
    first.start()
    cols = wv.shape[0]
    length = jnp.sqrt(colsq_ref[...] + 1e-06)
    basis = (right_ref[:cols, :].astype(F32) / length).astype(BF)
    bv[...] = basis
    second = pltpu.make_async_copy(bv, basis_ref, outs.at[1])
    second.start()
    coeff = 0.3 * (D * FF / RANK) ** 0.5 / 50.0
    update = jnp.dot(basis, ortho_ref[...], preferred_element_type=F32)
    wv[...] = (w_ref[...].astype(F32) - coeff * update).astype(BF)
    third = pltpu.make_async_copy(wv, weight_ref, outs.at[2])
    third.start()
    for cp in (first, second, third):
        cp.wait()


def vmem(n):
    return [pl.BlockSpec(memory_space=pltpu.VMEM)] * n


def anywhere(n):
    return [pl.BlockSpec(memory_space=pl.ANY)] * n


def bf(*shape):
    return jax.ShapeDtypeStruct(shape, BF)


def f32(*shape):
    return jax.ShapeDtypeStruct(shape, F32)


def per_device(sizes, weight, momentum, gradient, basis):
    nz, nx, ny, nc = sizes
    nloc, cols = momentum.shape
    q = nloc // nx
    th = RANK // nz
    h = RANK // 2
    dma = pltpu.SemaphoreType.DMA
    buft, power, gram = pl.pallas_call(
        functools.partial(power_kernel, sizes),
        out_shape=(bf(cols, nloc), bf(RANK, nloc), f32(RANK, RANK)),
        in_specs=anywhere(3),
        out_specs=tuple(vmem(3)),
        scratch_shapes=[
            pltpu.VMEM((cols, nloc), BF),
            pltpu.VMEM((cols, nloc), BF),
            pltpu.VMEM((cols, RANK), BF),
            pltpu.VMEM((RANK, nloc), BF),
            pltpu.VMEM((nx * nz, th, q), BF),
            pltpu.VMEM((nz, th, q), BF),
            pltpu.VMEM((nz, th, q), BF),
            pltpu.VMEM((RANK, nloc), BF),
            pltpu.VMEM((RANK, RANK), F32),
            pltpu.VMEM((h, RANK), F32),
            pltpu.VMEM((h, RANK), F32),
            pltpu.VMEM((ny, h // ny, RANK), F32),
            pltpu.VMEM((RANK, RANK), F32),
            dma((3,)), dma((nx * nz,)), dma((nx * nz,)),
            dma((nz,)), dma((nz,)), dma((nz,)), dma((nz,)), dma((nx,)), dma((nx,)),
            dma, dma, dma((ny,)), dma((ny,)), dma((ny,)), dma((ny,)), dma, dma,
        ],
        compiler_params=pltpu.CompilerParams(collective_id=0, has_side_effects=True),
    )(momentum.T, gradient.T, basis)

    sym, low, scale = pl.pallas_call(
        factor_kernel,
        out_shape=(f32(RANK, RANK), f32(RANK, RANK), f32(1, RANK)),
        in_specs=vmem(1),
        out_specs=tuple(vmem(3)),
        scratch_shapes=[pltpu.VMEM((RANK, RANK), F32)],
    )(gram)

    s = PAD // 2 // ny
    ortho, right, colsq, mom, held = pl.pallas_call(
        functools.partial(right_kernel, sizes),
        out_shape=(bf(RANK, nloc), bf(PAD, RANK), f32(1, RANK), bf(cols, nloc), bf(cols, nloc)),
        in_specs=vmem(5) + anywhere(1),
        out_specs=tuple(vmem(5)),
        scratch_shapes=[
            pltpu.VMEM((RANK, RANK), F32),
            pltpu.VMEM((PAD, RANK), BF),
            pltpu.VMEM((PAD // 2, RANK), BF),
            pltpu.VMEM((PAD // 2, RANK), BF),
            pltpu.VMEM((ny, s, RANK), BF),
            pltpu.VMEM((PAD, RANK), BF),
            pltpu.VMEM((ny * nx, 1, RANK), F32),
            pltpu.VMEM((nz * nc, 1, RANK), F32),
            dma, dma, dma, dma((ny,)), dma((ny,)), dma((ny,)), dma((ny,)), dma, dma,
            dma((ny * nx,)), dma((ny * nx,)), dma((nz * nc,)), dma((nz * nc,)),
        ],
        compiler_params=pltpu.CompilerParams(collective_id=1, has_side_effects=True),
    )(power, sym, low, scale, buft, weight.T)

    weight_new, momentum_new, basis_new = pl.pallas_call(
        update_kernel,
        out_shape=(bf(cols, nloc), bf(cols, nloc), bf(cols, RANK)),
        in_specs=vmem(5),
        out_specs=tuple(anywhere(3)),
        scratch_shapes=[pltpu.VMEM((cols, nloc), BF), pltpu.VMEM((cols, RANK), BF), dma((3,))],
    )(ortho, right, colsq, mom, held)
    return weight_new.T, momentum_new.T, basis_new


def build(devices, sizes):
    finer = Mesh(devices.reshape(sizes), (Z, X, Y, C))
    return jax.shard_map(
        functools.partial(per_device, sizes),
        mesh=finer,
        in_specs=(P(ROW, FSDP), P(ROW, FSDP), P(ROW, FSDP), P(FSDP, None)),
        out_specs=(P(ROW, FSDP), P(ROW, FSDP), P(FSDP, None)),
        check_vma=False,
    )


def solution(mesh):
    return build(mesh.devices, SIZES)
```

time: 147 us -> 135 us (0.918)
  Pallas kernels: 138 us -> 134 us
  matrix products: 3.24 us -> 0 us
  local copies, waits for them, and re-layouts: 3.1 us -> 0 us
  other arithmetic: 1.7 us -> 0 us
    pallas_call x3 -> x4, Pallas kernels: 138 us -> 134 us  [the longest x1 60.9 us: per_device(): pl.pallas_call(functools.partial(power_kernel, sizes), out_shape=(bf(cols...]
    dot_general x2 -> x0, matrix products: 3.24 us -> none  [the longest x1 2.17 us: per_device(): feedback = jnp.einsum('rk,ck->rc', ortho, whole, preferred_element_type=F32)]
    unnamed x12 -> x0, local copies, waits for them, and re-layouts: 3.1 us -> none
where the time goes in v2:
time: 135 us
  Pallas kernels  134 us (99%)
    pallas_call x1, Pallas kernels, per_device(): pl.pallas_call(functools.partial(power_kernel, sizes), out_shape=(bf(cols...  60.9 us
    pallas_call x1, Pallas kernels, per_device(): pl.pallas_call(factor_kernel, out_shape=(f32(RANK, RANK), f32(RANK, RANK)...  41 us
    pallas_call x1, Pallas kernels, per_device(): pl.pallas_call(functools.partial(right_kernel, sizes), out_shape=(bf(RANK...  29.7 us

profile of v2, /device:TPU:1, one launch (start us, length us, event | category | flops | bytes accessed | tf_op | source)
XLA Modules:
  0.0 134.5 jit_solution(9557144882236242037)
XLA Ops:
  0.6 60.9 %shard_map.67 = (bf16[416,512]{1,0:T(8,128)(2,1)}, bf16[256,512]{1,0:T(8,128)(2,1)}, f32[256,256]{1,0:T(8,128)}) custom-call(bf16[416,512]{1,0:T(8,128)(2,1)} %bitcast.5, bf16[416,512]{1,0:T(8,128)(2,1)} %bitcast.6, bf16[416,256]{1,0:T(8,128)(2,1)} %b_ref.1), custom_call_target="tpu_custom_call" | custom-call | tf_op jit(solution)/shard_map/pallas_call | solution.py:414
  61.5 41.0 %shard_map.68 = (f32[256,256]{1,0:T(8,128)}, f32[256,256]{1,0:T(8,128)}, f32[1,256]{1,0:T(1,128)}) custom-call(f32[256,256]{1,0:T(8,128)} %get-tuple-element.18.g_ref), custom_call_target="tpu_custom_call" | custom-call | tf_op jit(solution)/shard_map/pallas_call | solution.py:440
  102.5 29.7 %shard_map.69 = (bf16[256,512]{1,0:T(8,128)(2,1)}, bf16[512,256]{1,0:T(8,128)(2,1)}, f32[1,256]{1,0:T(1,128)}, bf16[416,512]{1,0:T(8,128)(2,1)}, bf16[416,512]{1,0:T(8,128)(2,1)}) custom-call(bf16[256,512]{1,0:T(8,128)(2,1)} %get-tuple-element.17.p_ref, f32[256,256]{1,0:T(8,128)} %get-tuple-element.19.sym, f32[256,256]{1,0:T(8,128)} %get-tuple-element.20.low_ref, ...), custom_call_target="tpu_custom_call" | custom-call | tf_op jit(solution)/shard_map/pallas_call | solution.py:449
  132.2 2.4 %shard_map.70 = (bf16[416,512]{1,0:T(8,128)(2,1)}, bf16[416,512]{1,0:T(8,128)(2,1)}, bf16[416,256]{1,0:T(8,128)(2,1)}) custom-call(bf16[256,512]{1,0:T(8,128)(2,1)} %get-tuple-element.23.ortho_ref, bf16[512,256]{1,0:T(8,128)(2,1)} %get-tuple-element.24.right_ref, f32[1,256]{1,0:T(1,128)} %get-tuple-element.25.colsq_ref, ...), custom_call_target="tpu_custom_call" | custom-call | tf_op jit(solution)/shard_map/pallas_call | solution.py:469

commit v3 on v2

v3 whole, which is shorter than its diff:
```python
import functools

import jax
import jax.numpy as jnp
from jax import lax
from jax.experimental import pallas as pl
from jax.experimental.pallas import tpu as pltpu
from jax.sharding import Mesh
from jax.sharding import PartitionSpec as P

D = 8192
FF = 26624
RANK = 256
Z, X, Y, C = "fsdp_0", "fsdp_1", "row_0", "row_1"
FSDP = (Z, X)
ROW = (Y, C)
SIZES = (16, 4, 8, 2)
BF, F32 = jnp.bfloat16, jnp.float32
PAD = 512
SMALL = 1e-2
MESH = pl.DeviceIdType.MESH


def far_first(n):
    return sorted(range(1, n), key=lambda d: -min(d, n - d))


def far_pairs(n, m):
    pairs = [(a, b) for a in range(n) for b in range(m) if a or b]
    return sorted(pairs, key=lambda p: -(min(p[0], n - p[0]) + min(p[1], m - p[1])))


def rows(start, size):
    return pl.ds(pl.multiple_of(start, size), size)


def wrap(i, n):
    return lax.rem(i, n)


def near_first(n):
    return far_first(n)[::-1]


def remote(src, dst, send, recv, peer):
    return pltpu.make_async_remote_copy(
        src_ref=src, dst_ref=dst, send_sem=send, recv_sem=recv, device_id=peer, device_id_type=MESH
    )


def lanes(a, b):
    return lax.dot_general(a, b, (((1,), (1,)), ((), ())), preferred_element_type=F32)


def full(a, b, dims):
    return lax.dot_general(
        a, b, (dims, ((), ())), precision=lax.Precision.HIGHEST, preferred_element_type=F32
    )


def quick(a, b, dims):
    return lax.dot_general(a.astype(BF), b.astype(BF), (dims, ((), ())), preferred_element_type=F32)


def square():
    n = RANK
    return (lax.broadcasted_iota(jnp.int32, (n, n), axis) for axis in (0, 1))


def newton_step(product, sym, low):
    i, j = square()
    inv = low[...]
    e = product(product(inv, sym[...], ((1,), (0,))), inv, ((1,), (1,)))
    e = e - jnp.where(i == j, 1.0, 0.0)
    phi = jnp.where(i > j, e, jnp.where(i == j, 0.5 * e, 0.0))
    low[...] = inv - product(phi, inv, ((1,), (0,)))
    return jnp.sum(e * e)


def fast_kernel(
    sizes, m_ref, g_ref, b_ref,
    buft_ref, p_ref, gram_ref, ortho_ref, right_ref, mom_ref, colsq_ref, err_ref,
    mv, gv, bv, buft, part, xbuf, zpart, zbuf, pbuf, gp, gbuf, gh, ybuf, gall, sym, low,
    obuf, rpart, cbuf, rhalf, wbuf, rall, sq1, sq2, mom,
    ins, store, xs, xr, zs, zr, zs2, zr2, xs2, xr2, cs, cr, ys, yr, ys2, yr2, cs2, cr2,
    cs3, cr3, ys3, yr3, ys4, yr4, cs4, cr4, s1, r1, s2, r2,
):
    nz, nx, ny, nc = sizes
    z, x, y, c = (lax.axis_index(a) for a in (Z, X, Y, C))
    loads = [pltpu.make_async_copy(a, b, ins.at[i]) for i, (a, b) in enumerate(((m_ref, mv), (g_ref, gv), (b_ref, bv)))]
    for cp in loads:
        cp.start()
    barrier = pltpu.get_barrier_semaphore()
    plane = far_pairs(ny, nx)
    line = far_pairs(nz, nc)
    for dz, dc in line:
        to = {Z: wrap(z + dz, nz), C: wrap(c + dc, nc)}
        pl.semaphore_signal(barrier, inc=1, device_id=to, device_id_type=MESH)
    for dy, dx in plane:
        to = {Y: wrap(y + dy, ny), X: wrap(x + dx, nx)}
        pl.semaphore_signal(barrier, inc=1, device_id=to, device_id_type=MESH)
    for cp in loads:
        cp.wait()

    buffer = (mv[...].astype(F32) + gv[...].astype(F32)).astype(BF)
    buft[...] = buffer
    part[...] = lax.dot_general(
        bv[...], buffer, (((0,), (0,)), ((), ())), preferred_element_type=F32
    ).astype(BF)
    outs = [pltpu.make_async_copy(buft, buft_ref, store.at[0])]
    outs[0].start()
    pl.semaphore_wait(barrier, len(plane) + len(line))

    q = part.shape[1] // nx
    th = RANK // nz
    order = far_first(nz) + [0]

    def tile(i, j):
        return (rows(i * th, th), rows(j * q, q))

    scatter = {}
    for e in order:
        to = wrap(z + e, nz)
        for d in far_first(nx):
            peer = wrap(x + d, nx)
            k = e * nx + d
            cp = remote(part.at[tile(to, peer)], xbuf.at[k], xs.at[k], xr.at[k], {X: peer})
            cp.start()
            scatter[k] = cp

    second = {}
    for e in order:
        to = wrap(z + e, nz)
        total = part[tile(to, x)].astype(F32)
        for d in far_first(nx):
            scatter[e * nx + d].wait_recv()
            total += xbuf[e * nx + d].astype(F32)
        if e:
            zpart[e] = total.astype(BF)
            second[e] = remote(zpart.at[e], zbuf.at[e], zs.at[e], zr.at[e], {Z: to})
            second[e].start()
        else:
            own = total
    for e in near_first(nz):
        second[e].wait_recv()
        own += zbuf[e].astype(F32)

    def forward(i):
        t = pbuf.at[tile(i, x)]
        for d in far_first(nx):
            remote(t, t, xs2.at[d], xr2.at[d], {X: wrap(x + d, nx)}).start()

    pbuf[tile(z, x)] = own.astype(BF)
    home = pbuf.at[tile(z, x)]
    gather = []
    for d in far_first(nz):
        cp = remote(home, home, zs2.at[d], zr2.at[d], {Z: wrap(z + d, nz)})
        cp.start()
        gather.append(cp)
    forward(z)
    for cp in list(scatter.values()) + list(second.values()):
        cp.wait_send()
    for d in near_first(nz):
        src = wrap(z - d + nz, nz)
        there = pbuf.at[tile(src, x)]
        remote(there, there, zs2.at[d], zr2.at[d], {Z: src}).wait_recv()
        forward(src)
    for cp in gather:
        cp.wait_send()

    def quarter(j):
        return (pl.ds(0, RANK), rows(j * q, q))

    for d in near_first(nx):
        src = wrap(x - d + nx, nx)
        there = pbuf.at[quarter(src)]
        remote(there, there, xs2.at[d], xr2.at[d], {X: src}).wait_recv()
    outs.append(pltpu.make_async_copy(pbuf, p_ref, store.at[1]))
    outs[1].start()
    b = RANK // 2
    gp[: 2 * b, :] = lanes(pbuf[...], pbuf[:b, :])
    gp[2 * b :, :] = lanes(pbuf[b:, :], pbuf[b:, :])

    h = 3 * b // 2
    peer = {C: 1 - c}
    cp = remote(gp.at[rows((1 - c) * h, h)], gbuf, cs, cr, peer)
    cp.start()
    for d in far_first(nx):
        mine = pbuf.at[quarter(x)]
        remote(mine, mine, xs2.at[d], xr2.at[d], {X: wrap(x + d, nx)}).wait_send()
    cp.wait()
    gh[...] = gp[rows(c * h, h), :] + gbuf[...]

    s = h // ny
    copies = []
    for d in far_first(ny):
        to = wrap(y + d, ny)
        cp = remote(gh.at[rows(to * s, s)], ybuf.at[d], ys.at[d], yr.at[d], {Y: to})
        cp.start()
        copies.append(cp)
    for cp in copies:
        cp.wait()
    own = gh[rows(y * s, s), :]
    for d in range(1, ny):
        own += ybuf[d]

    def slot(i):
        return rows(c * h + i * s, s)

    def across(i):
        t = gall.at[slot(i)]
        remote(t, t, cs2, cr2, peer).start()

    gall[slot(y), :] = own
    copies = []
    for d in far_first(ny):
        cp = remote(gall.at[slot(y)], gall.at[slot(y)], ys2.at[d], yr2.at[d], {Y: wrap(y + d, ny)})
        cp.start()
        copies.append(cp)
    across(y)
    for d in near_first(ny):
        src = wrap(y - d + ny, ny)
        remote(gall.at[slot(src)], gall.at[slot(src)], ys2.at[d], yr2.at[d], {Y: src}).wait_recv()
        across(src)
    for cp in copies:
        cp.wait_send()
    half = rows(c * h, h)
    remote(gall.at[half], gall.at[half], cs2, cr2, peer).wait_send()
    other = rows((1 - c) * h, h)
    remote(gall.at[other], gall.at[other], cs2, cr2, peer).wait_recv()
    outs.append(pltpu.make_async_copy(gall, gram_ref, store.at[2]))
    outs[2].start()

    corner = gall[b : 2 * b, :]
    sym[:b, :b] = gall[:b, :]
    sym[b:, :b] = corner
    sym[:b, b:] = corner.T
    sym[b:, b:] = gall[2 * b :, :]
    gram = sym[...]
    i, j = square()
    diag = jnp.where(i == j, gram, 0.0)
    scale = lax.rsqrt(jnp.sum(diag, axis=0, keepdims=True))
    down = lax.rsqrt(jnp.sum(diag, axis=1, keepdims=True))
    normed = gram * scale * down
    sym[...] = normed
    low[...] = jnp.where(i > j, -normed, jnp.where(i == j, 1.5 - 0.5 * normed, 0.0))
    newton_step(quick, sym, low)
    err_ref[...] = jnp.zeros((1, 128), F32) + newton_step(full, sym, low)
    inv = low[...] * scale
    hi = inv.astype(BF)
    lo = (inv - hi.astype(F32)).astype(BF)
    power = pbuf[...]
    ortho = jnp.dot(hi, power, preferred_element_type=F32)
    ortho += jnp.dot(lo, power, preferred_element_type=F32)
    ortho = ortho.astype(BF)
    obuf[...] = ortho
    outs.append(pltpu.make_async_copy(obuf, ortho_ref, store.at[3]))
    outs[3].start()
    cols = buft.shape[0]
    rpart[:cols, :] = lanes(buft[...], ortho).astype(BF)
    rpart[cols:, :] = jnp.zeros((PAD - cols, RANK), BF)

    h = PAD // 2
    peer = {C: 1 - c}
    cp = remote(rpart.at[rows((1 - c) * h, h)], cbuf, cs3, cr3, peer)
    cp.start()
    cp.wait()
    rhalf[...] = (rpart[rows(c * h, h), :].astype(F32) + cbuf[...].astype(F32)).astype(BF)

    s = h // ny
    copies = []
    for d in far_first(ny):
        to = wrap(y + d, ny)
        cp = remote(rhalf.at[rows(to * s, s)], wbuf.at[d], ys3.at[d], yr3.at[d], {Y: to})
        cp.start()
        copies.append(cp)
    for cp in copies:
        cp.wait()
    own = rhalf[rows(y * s, s), :].astype(F32)
    for d in range(1, ny):
        own += wbuf[d].astype(F32)

    sq1[0] = jnp.sum(own * own, axis=0, keepdims=True)
    first = []
    for dy, dx in plane:
        k = dy * nx + dx
        to = {Y: wrap(y + dy, ny), X: wrap(x + dx, nx)}
        cp = remote(sq1.at[0], sq1.at[k], s1.at[k], r1.at[k], to)
        cp.start()
        first.append(cp)

    def slot(i):
        return rows(c * h + i * s, s)

    rall[slot(y), :] = own.astype(BF)
    gather = []
    for d in far_first(ny):
        cp = remote(rall.at[slot(y)], rall.at[slot(y)], ys4.at[d], yr4.at[d], {Y: wrap(y + d, ny)})
        cp.start()
        gather.append(cp)

    for cp in first:
        cp.wait()
    sq2[0] = jnp.sum(sq1[...], axis=0)
    second = []
    for dz, dc in line:
        k = dz * nc + dc
        to = {Z: wrap(z + dz, nz), C: wrap(c + dc, nc)}
        cp = remote(sq2.at[0], sq2.at[k], s2.at[k], r2.at[k], to)
        cp.start()
        second.append(cp)

    for d, cp in zip(far_first(ny), gather):
        cp.wait_send()
        src = wrap(y - d + ny, ny)
        remote(rall.at[slot(src)], rall.at[slot(src)], ys4.at[d], yr4.at[d], {Y: src}).wait_recv()
    mine = rows(c * h, h)
    cp = remote(rall.at[mine], rall.at[mine], cs4, cr4, peer)
    cp.start()
    cp.wait_send()
    other = rows((1 - c) * h, h)
    remote(rall.at[other], rall.at[other], cs4, cr4, peer).wait_recv()
    outs.append(pltpu.make_async_copy(rall, right_ref, store.at[4]))
    outs[4].start()
    feedback = jnp.dot(rall[:cols, :], ortho, preferred_element_type=F32)
    mom[...] = (buft[...].astype(F32) - 0.5 * feedback).astype(BF)
    outs.append(pltpu.make_async_copy(mom, mom_ref, store.at[5]))
    outs[5].start()
    for cp in second:
        cp.wait()
    colsq_ref[...] = jnp.sum(sq2[...], axis=0)
    for cp in outs:
        cp.wait()


def direct_kernel(g_ref, inv_ref, work):
    n = RANK
    i, j = square()
    gram = g_ref[...]
    diag = jnp.where(i == j, gram, 0.0)
    across = lax.rsqrt(jnp.sum(diag, axis=0, keepdims=True))
    down = lax.rsqrt(jnp.sum(diag, axis=1, keepdims=True))
    work[...] = gram * across * down
    inv_ref[...] = jnp.where(i == j, 1.0, 0.0)
    lane = lax.broadcasted_iota(jnp.int32, (1, n), 1)
    line = lax.broadcasted_iota(jnp.int32, (n, 1), 0)

    def column(k, _):
        pivots = work[pl.ds(k, 1), :]
        pivot = jnp.sum(jnp.where(lane == k, pivots, 0.0), axis=1, keepdims=True)
        inverse = inv_ref[pl.ds(k, 1), :]
        here = work[...]
        col = jnp.sum(jnp.where(j == k, here, 0.0), axis=1, keepdims=True)
        times = jnp.where(line > k, col / pivot, 0.0)
        work[...] = here - times * pivots
        inv_ref[...] = inv_ref[...] - times * inverse
        return 0

    lax.fori_loop(0, n, column, 0)
    pivot = jnp.sum(jnp.where(i == j, work[...], 0.0), axis=1, keepdims=True)
    inv_ref[...] = inv_ref[...] * lax.rsqrt(pivot) * across


def update_kernel(
    ortho_ref, right_ref, colsq_ref, mom_ref, w_ref, weight_ref, momentum_ref, basis_ref, wv, bv, outs
):
    first = pltpu.make_async_copy(mom_ref, momentum_ref, outs.at[0])
    first.start()
    cols = wv.shape[0]
    length = jnp.sqrt(colsq_ref[...] + 1e-06)
    basis = (right_ref[:cols, :].astype(F32) / length).astype(BF)
    bv[...] = basis
    second = pltpu.make_async_copy(bv, basis_ref, outs.at[1])
    second.start()
    coeff = 0.3 * (D * FF / RANK) ** 0.5 / 50.0
    update = jnp.dot(basis, ortho_ref[...], preferred_element_type=F32)
    wv[...] = (w_ref[...].astype(F32) - coeff * update).astype(BF)
    third = pltpu.make_async_copy(wv, weight_ref, outs.at[2])
    third.start()
    for cp in (first, second, third):
        cp.wait()


def vmem(n):
    return [pl.BlockSpec(memory_space=pltpu.VMEM)] * n


def anywhere(n):
    return [pl.BlockSpec(memory_space=pl.ANY)] * n


def bf(*shape):
    return jax.ShapeDtypeStruct(shape, BF)


def f32(*shape):
    return jax.ShapeDtypeStruct(shape, F32)


def finish(ortho, right, colsq, mom, weight):
    cols, nloc = mom.shape
    return pl.pallas_call(
        update_kernel,
        out_shape=(bf(cols, nloc), bf(cols, nloc), bf(cols, RANK)),
        in_specs=vmem(5),
        out_specs=tuple(anywhere(3)),
        scratch_shapes=[pltpu.VMEM((cols, nloc), BF), pltpu.VMEM((cols, RANK), BF), pltpu.SemaphoreType.DMA((3,))],
    )(ortho, right, colsq, mom, weight)


def general(sizes, buft, power, gram, weight):
    b = RANK // 2
    corner = gram[b : 2 * b]
    upper = jnp.concatenate([gram[:b], corner.T], axis=1)
    lower = jnp.concatenate([corner, gram[2 * b :]], axis=1)
    inv = pl.pallas_call(
        direct_kernel,
        out_shape=f32(RANK, RANK),
        in_specs=vmem(1),
        out_specs=vmem(1)[0],
        scratch_shapes=[pltpu.VMEM((RANK, RANK), F32)],
    )(jnp.concatenate([upper, lower]))
    hi = inv.astype(BF)
    lo = (inv - hi.astype(F32)).astype(BF)
    ortho = jnp.dot(hi, power, preferred_element_type=F32)
    ortho = (ortho + jnp.dot(lo, power, preferred_element_type=F32)).astype(BF)
    right = jnp.einsum("cr,kr->ck", buft, ortho, preferred_element_type=F32)
    pieces = right.reshape(sizes[2] * sizes[3], -1, RANK)
    share = jnp.sum(lax.all_to_all(pieces, ROW, 0, 0, tiled=True), axis=0)
    whole = lax.all_gather(share.astype(BF), ROW, tiled=True)
    colsq = jnp.sum(share * share, axis=0, keepdims=True)
    colsq = jnp.sum(lax.all_gather(colsq, ROW, tiled=True), axis=0, keepdims=True)
    colsq = jnp.sum(lax.all_gather(colsq, FSDP, tiled=True), axis=0, keepdims=True)
    feedback = jnp.dot(whole, ortho, preferred_element_type=F32)
    mom = (buft.astype(F32) - 0.5 * feedback).astype(BF)
    whole = jnp.pad(whole, ((0, PAD - whole.shape[0]), (0, 0)))
    return finish(ortho, whole, colsq, mom, weight)


def per_device(sizes, weight, momentum, gradient, basis):
    nz, nx, ny, nc = sizes
    nloc, cols = momentum.shape
    q = nloc // nx
    th = RANK // nz
    b = RANK // 2
    h = 3 * b // 2
    s = PAD // 2 // ny
    dma = pltpu.SemaphoreType.DMA
    scratch = [
        bf(cols, nloc), bf(cols, nloc), bf(cols, RANK), bf(cols, nloc), bf(RANK, nloc),
        bf(nx * nz, th, q), bf(nz, th, q), bf(nz, th, q), bf(RANK, nloc),
        f32(3 * b, b), f32(h, b), f32(h, b), f32(ny, h // ny, b), f32(3 * b, b), f32(RANK, RANK), f32(RANK, RANK),
        bf(RANK, nloc), bf(PAD, RANK), bf(PAD // 2, RANK), bf(PAD // 2, RANK), bf(ny, s, RANK), bf(PAD, RANK),
        f32(ny * nx, 1, RANK), f32(nz * nc, 1, RANK), bf(cols, nloc),
    ]
    buft, power, gram, ortho, right, mom, colsq, err = pl.pallas_call(
        functools.partial(fast_kernel, sizes),
        out_shape=(
            bf(cols, nloc), bf(RANK, nloc), f32(3 * b, b), bf(RANK, nloc), bf(PAD, RANK), bf(cols, nloc),
            f32(1, RANK), f32(1, 128),
        ),
        in_specs=anywhere(3),
        out_specs=tuple(anywhere(6) + vmem(2)),
        scratch_shapes=[pltpu.VMEM(v.shape, v.dtype) for v in scratch] + [
            dma((3,)), dma((6,)), dma((nx * nz,)), dma((nx * nz,)),
            dma((nz,)), dma((nz,)), dma((nz,)), dma((nz,)), dma((nx,)), dma((nx,)),
            dma, dma, dma((ny,)), dma((ny,)), dma((ny,)), dma((ny,)), dma, dma,
            dma, dma, dma((ny,)), dma((ny,)), dma((ny,)), dma((ny,)), dma, dma,
            dma((ny * nx,)), dma((ny * nx,)), dma((nz * nc,)), dma((nz * nc,)),
        ],
        compiler_params=pltpu.CompilerParams(collective_id=0, has_side_effects=True),
    )(momentum.T, gradient.T, basis)

    weight_new, momentum_new, basis_new = lax.cond(
        err[0, 0] <= SMALL,
        lambda: finish(ortho, right, colsq, mom, weight.T),
        lambda: general(sizes, buft, power, gram, weight.T),
    )
    return weight_new.T, momentum_new.T, basis_new


def build(devices, sizes):
    finer = Mesh(devices.reshape(sizes), (Z, X, Y, C))
    return jax.shard_map(
        functools.partial(per_device, sizes),
        mesh=finer,
        in_specs=(P(ROW, FSDP), P(ROW, FSDP), P(ROW, FSDP), P(FSDP, None)),
        out_specs=(P(ROW, FSDP), P(ROW, FSDP), P(FSDP, None)),
        check_vma=False,
    )


def solution(mesh):
    return build(mesh.devices, SIZES)
```

time: 135 us -> 266 us (1.97)
  blocking collectives: 0 us -> 132 us
  Pallas kernels: 134 us -> 126 us
  matrix products: 0 us -> 2.79 us
    all_gather x0 -> x3, blocking collectives: none -> 110 us  [the longest x1 61.6 us: general(): lax.all_gather(colsq, FSDP, tiled=True)]
    all_to_all x0 -> x1, blocking collectives: none -> 22.1 us  [general(): share = jnp.sum(lax.all_to_all(pieces, ROW, 0, 0, tiled=True), axis=0)]
    pallas_call x4 -> x3, Pallas kernels: 134 us -> 126 us  [the longest x1 85.3 us: per_device(): pl.pallas_call(functools.partial(fast_kernel, sizes), out_shape=(bf(cols,...]
    dot_general x0 -> x4, matrix products: none -> 2.79 us  [the longest x1 1.24 us: general(): ortho = jnp.dot(hi, power, preferred_element_type=F32)]
where the time goes in v3:
time: 266 us
  blocking collectives  132 us (50%)
  Pallas kernels  126 us (47%)
  matrix products  2.79 us (1%)
    pallas_call x1, Pallas kernels, per_device(): pl.pallas_call(functools.partial(fast_kernel, sizes), out_shape=(bf(cols,...  85.3 us
    all_gather x1, blocking collectives, general(): lax.all_gather(colsq, FSDP, tiled=True)  61.6 us
    pallas_call x1, Pallas kernels, general(): pl.pallas_call(direct_kernel, out_shape=f32(RANK, RANK), in_specs=vmem(1)...  39 us
    all_gather x1, blocking collectives, general(): whole = lax.all_gather(share.astype(BF), ROW, tiled=True)  34.2 us
    all_to_all x1, blocking collectives, general(): share = jnp.sum(lax.all_to_all(pieces, ROW, 0, 0, tiled=True), axis=0)  22.1 us
    all_gather x1, blocking collectives, general(): lax.all_gather(colsq, ROW, tiled=True)  14.5 us

profile of v3, /device:TPU:1, one launch (start us, length us, event | category | flops | bytes accessed | tf_op | source)
XLA Modules:
  0.0 265.7 jit_solution(14451948203568663219)
XLA Ops:
  0.6 0.0 copy-start.2
  0.6 85.3 %shard_map.67 = (bf16[416,512]{1,0:T(8,128)(2,1)S(1)}, bf16[256,512]{1,0:T(8,128)(2,1)S(1)}, f32[384,128]{1,0:T(8,128)S(1)}, bf16[256,512]{1,0:T(8,128)(2,1)S(1)...) custom-call(bf16[416,512]{1,0:T(8,128)(2,1)} %bitcast.25, ...), custom_call_target="tpu_custom_call" | custom-call | tf_op jit(solution)/shard_map/pallas_call | solution.py:456
  85.9 0.0 copy-start.3
  85.9 0.7 copy-done.3
  86.6 0.0 copy-done.2
  86.6 179.1 %conditional.1 = ((bf16[416,512]{1,0:T(8,128)(2,1)}, bf16[416,512]{1,0:T(8,128)(2,1)}, bf16[416,256]{1,0:T(8,128)(2,1)})) conditional(s32[]{:T(128)} %bitcast.10, (f32[384,128]{1,0:T(8,128)S(1)}, bf16[256,512]{1,0:T(8,128)(2,1)S(1)}, bf16[416,512]{1,0:T(8,128)(2,1)S(1)}, bf16[512,416]{0,1:T(8,128)(2,1)S(1)}) %tuple.24, ...), branch_computations={%region_0.5_spmd, %region_5.6_spmd} | conditional | flops 354066688 | bytes 12291150 | solution.py:474
  86.7 0.1 copy.11
  86.8 0.1 copy.12
  86.9 0.7 maximum_maximum_fusion.g_ref
  87.7 39.0 %branch_0_fun.2 = f32[256,256]{1,0:T(8,128)} custom-call(f32[256,256]{1,0:T(8,128)} %maximum_maximum_fusion.g_ref), custom_call_target="tpu_custom_call" | custom-call | tf_op jit(solution)/shard_map/cond/branch_0_fun/pallas_call | solution.py:416
  126.6 0.0 copy-start.1
  126.6 1.2 fusion.4
  127.9 0.0 copy-done.1
  127.9 0.2 fusion.2.ortho_ref
  128.1 0.0 copy-start
  128.1 0.3 convolution_bitcast_fusion
  128.4 0.1 reshape.12
  128.5 22.1 %all_to_all.4 = f32[16,26,256]{2,1,0:T(8,128)S(1)} all-to-all(f32[16,26,256]{2,1,0:T(8,128)S(1)} %reshape.12), channel_id=1, replica_groups=mesh['fsdp_0'=16,'fsdp_1'=4,'row_0'=8,'row_1'=2] {'row_0','row_1'}, dimensions={0} | all-to-all | bytes 851968 | tf_op jit(solution)/shard_map/cond/branch_0_fun/all_to_all | solution.py:429
  150.7 14.5 %all-gather.3 = f32[16,1,256]{2,1,0:T(1,128)S(1)} all-gather(f32[1,1,256]{2,1,0:T(1,128)S(1)} %bitcast.29), channel_id=2, replica_groups=mesh['fsdp_0'=16,'fsdp_1'=4,'row_0'=8,'row_1'=2] {'row_0','row_1'}, dimensions={0}, use_global_device_ids=true | all-gather | bytes 17408 | tf_op jit(solution)/shard_map/cond/branch_0_fun/all_gather | solution.py:432
  165.2 61.6 %all-gather.4 = f32[64,1,256]{2,1,0:T(1,128)S(1)} all-gather(f32[1,1,256]{2,1,0:T(1,128)S(1)} %bitcast.28), channel_id=3, replica_groups=mesh['fsdp_0'=16,'fsdp_1'=4,'row_0'=8,'row_1'=2] {'fsdp_0','fsdp_1'}, dimensions={0}, use_global_device_ids=true | all-gather | bytes 66560 | tf_op jit(solution)/shard_map/cond/branch_0_fun/all_gather | solution.py:433
  226.8 0.7 reduce_sum.35
  227.5 34.2 %all-gather.2 = bf16[16,26,256]{2,1,0:T(8,128)(2,1)S(1)} all-gather(bf16[1,26,256]{2,1,0:T(8,128)(2,1)S(1)} %get-tuple-element.56), channel_id=1, replica_groups=mesh['fsdp_0'=16,'fsdp_1'=4,'row_0'=8,'row_1'=2] {'row_0','row_1'}, dimensions={0}, use_global_device_ids=true | all-gather | bytes 226304 | tf_op jit(solution)/shard_map/cond/branch_0_fun/all_gather | solution.py:430
  261.6 0.1 reshape.17
  261.7 0.0 copy-done
  261.7 1.0 fusion.1.mom_ref
  262.7 0.7 pad.3.right_ref
  263.5 2.2 branch_0_fun.3
  (6 shorter events, 0.1 us)
Async XLA Ops:
  0.6 86.0 %copy-start.2 = (bf16[512,416]{0,1:T(8,128)(2,1)S(1)}, bf16[512,416]{0,1:T(8,128)(2,1)}, u32[]{:S(2)}) copy-start(bf16[512,416]{0,1:T(8,128)(2,1)} %param.6) | copy-start | bytes 1277956
  85.9 0.7 copy-start.3
  126.6 1.3 copy-start.1
  128.1 133.6 %copy-start = (bf16[256,512]{1,0:T(8,128)(2,1)}, bf16[256,512]{1,0:T(8,128)(2,1)S(1)}, u32[]{:S(2)}) copy-start(bf16[256,512]{1,0:T(8,128)(2,1)S(1)} %fusion.2.ortho_ref) | copy-start | bytes 786436 | tf_op jit(solution)/shard_map/cond

commit v4 on v3

--- a/solution.py
+++ b/solution.py
@@ -292,13 +292,6 @@
     def slot(i):
         return rows(c * h + i * s, s)
 
-    rall[slot(y), :] = own.astype(BF)
-    gather = []
-    for d in far_first(ny):
-        cp = remote(rall.at[slot(y)], rall.at[slot(y)], ys4.at[d], yr4.at[d], {Y: wrap(y + d, ny)})
-        cp.start()
-        gather.append(cp)
-
     for cp in first:
         cp.wait()
     sq2[0] = jnp.sum(sq1[...], axis=0)
@@ -309,6 +302,13 @@
         cp = remote(sq2.at[0], sq2.at[k], s2.at[k], r2.at[k], to)
         cp.start()
         second.append(cp)
+
+    rall[slot(y), :] = own.astype(BF)
+    gather = []
+    for d in far_first(ny):
+        cp = remote(rall.at[slot(y)], rall.at[slot(y)], ys4.at[d], yr4.at[d], {Y: wrap(y + d, ny)})
+        cp.start()
+        gather.append(cp)
 
     for d, cp in zip(far_first(ny), gather):
         cp.wait_send()

time: 266 us -> 266 us (level)
  no operation moved by 1% of the time
where the time goes in v4:
time: 266 us
  blocking collectives  132 us (50%)
  Pallas kernels  126 us (47%)
  matrix products  2.8 us (1%)
    pallas_call x1, Pallas kernels, per_device(): pl.pallas_call(functools.partial(fast_kernel, sizes), out_shape=(bf(cols,...  85.2 us
    all_gather x1, blocking collectives, general(): lax.all_gather(colsq, FSDP, tiled=True)  61.6 us
    pallas_call x1, Pallas kernels, general(): pl.pallas_call(direct_kernel, out_shape=f32(RANK, RANK), in_specs=vmem(1)...  39 us
    all_gather x1, blocking collectives, general(): whole = lax.all_gather(share.astype(BF), ROW, tiled=True)  34.2 us
    all_to_all x1, blocking collectives, general(): share = jnp.sum(lax.all_to_all(pieces, ROW, 0, 0, tiled=True), axis=0)  22.1 us
    all_gather x1, blocking collectives, general(): lax.all_gather(colsq, ROW, tiled=True)  14.5 us

profile of v4, /device:TPU:1, one launch (start us, length us, event | category | flops | bytes accessed | tf_op | source)
XLA Modules:
  0.0 265.7 jit_solution(2791532060799902565)
XLA Ops:
  0.6 0.0 copy-start.2
  0.6 85.2 %shard_map.67 = (bf16[416,512]{1,0:T(8,128)(2,1)S(1)}, bf16[256,512]{1,0:T(8,128)(2,1)S(1)}, f32[384,128]{1,0:T(8,128)S(1)}, bf16[256,512]{1,0:T(8,128)(2,1)S(1)...) custom-call(bf16[416,512]{1,0:T(8,128)(2,1)} %bitcast.25, ...), custom_call_target="tpu_custom_call" | custom-call | tf_op jit(solution)/shard_map/pallas_call | solution.py:456
  85.8 0.0 copy-start.3
  85.8 0.7 copy-done.3
  86.5 0.0 copy-done.2
  86.5 179.1 %conditional.1 = ((bf16[416,512]{1,0:T(8,128)(2,1)}, bf16[416,512]{1,0:T(8,128)(2,1)}, bf16[416,256]{1,0:T(8,128)(2,1)})) conditional(s32[]{:T(128)} %bitcast.10, (f32[384,128]{1,0:T(8,128)S(1)}, bf16[256,512]{1,0:T(8,128)(2,1)S(1)}, bf16[416,512]{1,0:T(8,128)(2,1)S(1)}, bf16[512,416]{0,1:T(8,128)(2,1)S(1)}) %tuple.24, ...), branch_computations={%region_0.5_spmd, %region_5.6_spmd} | conditional | flops 354066688 | bytes 12291150 | solution.py:474
  86.6 0.1 copy.11
  86.7 0.1 copy.12
  86.8 0.7 maximum_maximum_fusion.g_ref
  87.6 39.0 %branch_0_fun.2 = f32[256,256]{1,0:T(8,128)} custom-call(f32[256,256]{1,0:T(8,128)} %maximum_maximum_fusion.g_ref), custom_call_target="tpu_custom_call" | custom-call | tf_op jit(solution)/shard_map/cond/branch_0_fun/pallas_call | solution.py:416
  126.5 0.0 copy-start.1
  126.5 1.2 fusion.4
  127.8 0.0 copy-done.1
  127.8 0.2 fusion.2.ortho_ref
  128.0 0.0 copy-start
  128.0 0.3 convolution_bitcast_fusion
  128.3 0.1 reshape.12
  128.4 22.1 %all_to_all.4 = f32[16,26,256]{2,1,0:T(8,128)S(1)} all-to-all(f32[16,26,256]{2,1,0:T(8,128)S(1)} %reshape.12), channel_id=1, replica_groups=mesh['fsdp_0'=16,'fsdp_1'=4,'row_0'=8,'row_1'=2] {'row_0','row_1'}, dimensions={0} | all-to-all | bytes 851968 | tf_op jit(solution)/shard_map/cond/branch_0_fun/all_to_all | solution.py:429
  150.6 14.5 %all-gather.3 = f32[16,1,256]{2,1,0:T(1,128)S(1)} all-gather(f32[1,1,256]{2,1,0:T(1,128)S(1)} %bitcast.29), channel_id=2, replica_groups=mesh['fsdp_0'=16,'fsdp_1'=4,'row_0'=8,'row_1'=2] {'row_0','row_1'}, dimensions={0}, use_global_device_ids=true | all-gather | bytes 17408 | tf_op jit(solution)/shard_map/cond/branch_0_fun/all_gather | solution.py:432
  165.1 61.6 %all-gather.4 = f32[64,1,256]{2,1,0:T(1,128)S(1)} all-gather(f32[1,1,256]{2,1,0:T(1,128)S(1)} %bitcast.28), channel_id=3, replica_groups=mesh['fsdp_0'=16,'fsdp_1'=4,'row_0'=8,'row_1'=2] {'fsdp_0','fsdp_1'}, dimensions={0}, use_global_device_ids=true | all-gather | bytes 66560 | tf_op jit(solution)/shard_map/cond/branch_0_fun/all_gather | solution.py:433
  226.7 0.7 reduce_sum.35
  227.4 34.2 %all-gather.2 = bf16[16,26,256]{2,1,0:T(8,128)(2,1)S(1)} all-gather(bf16[1,26,256]{2,1,0:T(8,128)(2,1)S(1)} %get-tuple-element.56), channel_id=1, replica_groups=mesh['fsdp_0'=16,'fsdp_1'=4,'row_0'=8,'row_1'=2] {'row_0','row_1'}, dimensions={0}, use_global_device_ids=true | all-gather | bytes 226304 | tf_op jit(solution)/shard_map/cond/branch_0_fun/all_gather | solution.py:430
  261.6 0.1 reshape.17
  261.7 0.0 copy-done
  261.7 1.0 fusion.1.mom_ref
  262.7 0.7 pad.3.right_ref
  263.4 2.2 branch_0_fun.3
  (6 shorter events, 0.1 us)
Async XLA Ops:
  0.6 85.9 %copy-start.2 = (bf16[512,416]{0,1:T(8,128)(2,1)S(1)}, bf16[512,416]{0,1:T(8,128)(2,1)}, u32[]{:S(2)}) copy-start(bf16[512,416]{0,1:T(8,128)(2,1)} %param.6) | copy-start | bytes 1277956
  85.8 0.7 copy-start.3
  126.5 1.3 copy-start.1
  128.0 133.6 %copy-start = (bf16[256,512]{1,0:T(8,128)(2,1)}, bf16[256,512]{1,0:T(8,128)(2,1)S(1)}, u32[]{:S(2)}) copy-start(bf16[256,512]{1,0:T(8,128)(2,1)S(1)} %fusion.2.ortho_ref) | copy-start | bytes 786436 | tf_op jit(solution)/shard_map/cond
